TPU v7x, 128 devices: a whole 4x4x4 slice. The times are simulated.
128 devices in a mesh: ctx: 8 (over z, x_lo), tp: 4 (over x_hi, core), dp: 4 (over y).
Axes of the slice: x: 4 (x_hi: 2, x_lo: 2; x = x_hi * 2 + x_lo), y: 4, z: 4, core: 2. Of those that a mesh axis runs over, the one named last changes fastest.
Arguments:
- hidden: bfloat16 [4, 4096, 4096], P('dp', 'ctx', 'tp'), may hold values from -6 to 6
- target: bfloat16 [4, 4096, 4096], P('dp', 'ctx', 'tp'), may hold values from -24 to 24
- gain: float32 [4096], replicated, may hold values from 0.5 to 1.5
- w_query: bfloat16 [4096, 2048], P(('ctx', 'dp'), 'tp'), may hold values from -2.15625 to 2.15625
- w_key: bfloat16 [4096, 512], P(('ctx', 'dp'), 'tp'), may hold values from -0.09375 to 0.09375
- value_matrix: bfloat16 [4096, 512], P(('ctx', 'dp'), 'tp'), may hold values from -0.09375 to 0.09375
- w_out: bfloat16 [2048, 4096], P('tp', ('ctx', 'dp')), may hold values from -0.125 to 0.125
- block_order: int32 [16], replicated, may hold values from 0 to 15, each once
Outputs:
- branch: bfloat16 [4, 4096, 4096], P('dp', 'ctx', 'tp')
- loss: float32 [], replicated
Inputs may be any that keep to these rules, and one draw needn't show every extreme that they name: block_order is a permutation of 0 to 15.
All inputs are finite; a program needn't handle non-finite values.
Results may differ from a plain program's by a relative error of at most 0.013.
The roundings to bfloat16 on the way count: a program that leaves them out, or rounds other values in their place, can miss the bound.
Values may be sent and summed in bfloat16 or wider, within the bound.
A program may use at most 128 MiB of HBM per device.

v0:
```python
import jax
import jax.numpy as jnp
from jax import lax
from jax.sharding import Mesh
from jax.sharding import PartitionSpec as P

MODEL_WIDTH = 4096
QUERY_HEADS = 16
KEY_VALUE_HEADS = 4
HEAD_SIZE = 128
TP = ("tp_0", "tp_1")
CTX_DP = ("ctx_0", "ctx_1", "dp")
CTX = ("ctx_0", "ctx_1")
CTX_TP_DP = ("ctx_0", "ctx_1", "tp_0", "tp_1", "dp")


rope_base = 500000.0


def side_by_side(arrays, axis, dim, along):
    widths = [a.shape[along] for a in arrays]
    both = jnp.concatenate(arrays, axis=along)
    whole = lax.all_gather(both, axis, axis=dim, tiled=True)
    return tuple(jnp.split(whole, [sum(widths[:k]) for k in range(1, len(widths))], axis=along))


def shifted(value, axis, by):
    peers = lax.axis_size(axis)
    return lax.ppermute(value, axis, [(i, (i + by) % peers) for i in range(peers)])


def by_axis(value, axes):
    for axis in axes:
        value = lax.psum(value, axis)
    return value


def positions(order, start, rows, half):
    index = start + lax.iota(jnp.int32, rows)
    block = index // half
    slots = lax.iota(jnp.int32, order.shape[0])
    chosen = jnp.sum(jnp.where(block[:, None] == slots[None, :], order[None, :], 0), axis=1)
    return chosen * half + index % half


def apply_rotary(values, token_places):
    half = values.shape[-1] // 2
    freqs = rope_base ** (-(jnp.arange(half, dtype=jnp.float32) * 2.0) / values.shape[-1])
    angles = token_places.astype(jnp.float32)[:, None] * freqs[None, :]
    cosine = jnp.cos(angles)[:, None, :]
    sine = jnp.sin(angles)[:, None, :]
    first = values[..., :half]
    second = values[..., half:]
    return jnp.concatenate(
        [first * cosine - second * sine, second * cosine + first * sine], axis=-1
    )


def attend(state, query_rows, qpos, piece, kpos):
    peak, total, accum = state
    rows = piece.shape[1]
    local_heads = query_rows.shape[1]
    pair = piece.reshape(2, rows, local_heads, HEAD_SIZE)
    scores = jnp.einsum(
        "qcgd,kcd->cgqk", query_rows, pair[0], preferred_element_type=jnp.float32
    ) * (1.0 / HEAD_SIZE**0.5)
    allowed = (qpos[:, None] >= kpos[None, :])[None, None]
    scores = jnp.where(allowed, scores, -1e30)
    new_peak = jnp.maximum(peak, jnp.max(scores, axis=-1))
    weights = jnp.where(allowed, jnp.exp(scores - new_peak[..., None]), 0.0)
    factor = jnp.exp(peak - new_peak)
    total = total * factor + jnp.sum(weights, axis=-1)
    update = jnp.einsum(
        "cgqk,kcd->qcgd", weights.astype(jnp.bfloat16), pair[1], preferred_element_type=jnp.float32
    )
    accum = accum * jnp.transpose(factor, (2, 0, 1))[..., None] + update
    return (new_peak, total, accum)


def on_device(hidden, target, gain, w_query, w_key, value_matrix, w_out, block_order):
    rows = hidden.shape[1]
    half = rows // 2
    local = hidden[0]
    whole = lax.all_gather(local, TP, axis=1, tiled=True)
    wide = whole.astype(jnp.float32)
    normed = (
        wide * lax.rsqrt(jnp.mean(wide * wide, axis=1, keepdims=True) + 1e-05) * gain[None, :]
    ).astype(jnp.bfloat16)
    pieces = side_by_side((w_query, w_key, value_matrix), CTX_DP, 0, 1)
    query_rows, key, value_rows = tuple(
        (jnp.dot(normed, piece, preferred_element_type=jnp.float32) for piece in pieces)
    )
    shard = lax.axis_index(CTX)
    qpos = positions(block_order, shard * rows, rows, half)
    local_heads = w_key.shape[1] // HEAD_SIZE
    query_group = QUERY_HEADS // KEY_VALUE_HEADS
    query_rows = (
        apply_rotary(query_rows.reshape(rows, local_heads * query_group, HEAD_SIZE), qpos)
        .astype(jnp.bfloat16)
        .reshape(rows, local_heads, query_group, HEAD_SIZE)
    )
    key = (
        apply_rotary(key.reshape(rows, local_heads, HEAD_SIZE), qpos)
        .astype(jnp.bfloat16)
        .reshape(rows, local_heads * HEAD_SIZE)
    )
    pair = jnp.stack([key, value_rows.astype(jnp.bfloat16)])
    state = (
        jnp.full((local_heads, query_group, rows), -1e30, jnp.float32),
        jnp.zeros((local_heads, query_group, rows), jnp.float32),
        jnp.zeros((rows, local_heads, query_group, HEAD_SIZE), jnp.float32),
    )
    count = lax.axis_size(CTX)
    state = attend(state, query_rows, qpos, pair, qpos)

    def turn(step, carry):
        moved, inner = carry
        moved = shifted(moved, CTX, 1)
        source = (shard - step) % count
        return (
            moved,
            attend(
                inner, query_rows, qpos, moved, positions(block_order, source * rows, rows, half)
            ),
        )

    moved_end, state = lax.fori_loop(1, count, turn, (pair, state))
    peak, total, accum = state
    attn = (
        (accum / jnp.transpose(total, (2, 0, 1))[..., None])
        .astype(jnp.bfloat16)
        .reshape(rows, local_heads * query_group * HEAD_SIZE)
    )
    terms = jnp.dot(
        attn, lax.all_gather(w_out, CTX_DP, axis=1, tiled=True), preferred_element_type=jnp.float32
    )
    summed = lax.psum_scatter(terms.astype(jnp.bfloat16), TP, scatter_dimension=1, tiled=True)
    resid = local.astype(jnp.float32) + summed.astype(jnp.float32) - target[0].astype(jnp.float32)
    squares = by_axis(jnp.sum(resid * resid), CTX_TP_DP)
    loss = squares / (lax.axis_size("dp") * lax.axis_size(CTX) * rows * MODEL_WIDTH)
    return (summed[None], loss)


def solution(mesh):
    split = Mesh(
        mesh.devices.reshape(4, 2, 2, 2, mesh.shape["dp"]), ("ctx_0", "ctx_1", "tp_0", "tp_1", "dp")
    )
    placed = (
        P("dp", CTX, TP),
        P("dp", CTX, TP),
        P(),
        P(CTX_DP, TP),
        P(CTX_DP, TP),
        P(CTX_DP, TP),
        P(TP, CTX_DP),
        P(),
    )
    return jax.shard_map(
        on_device, mesh=split, in_specs=placed, out_specs=(P("dp", CTX, TP), P()), check_vma=False
    )
```

profile of v0, /device:TPU:1, one launch (start us, length us, event | category | flops | bytes accessed | tf_op | source)
XLA Modules:
  0.0 469.5 jit_solution(3761613661042491289)
XLA Ops:
  12.4 39.4 %all-gather.9.cloned.1.call-done = bf16[1,512,4096]{2,1,0:T(8,128)(2,1)} async-done(((bf16[1,512,1024]{2,1,0:T(8,128)(2,1)}), bf16[1,512,4096]{2,1,0:T(8,128)(2,1)}) %all-gather.9.cloned.1.call-update) | async-done | bytes 4194320 | tf_op jit(solution)/shard_map/all_gather | solution.py:84
  51.8 3.1 fusion.23
  54.9 139.6 %all-gather.5.cloned.1.call-done = bf16[4096,768]{1,0:T(8,128)(2,1)} async-done(((bf16[128,768]{1,0:T(8,128)(2,1)}), bf16[4096,768]{1,0:T(8,128)(2,1)}) %all-gather.5.cloned.1.call-update) | async-done | bytes 6291472 | tf_op jit(solution)/shard_map/all_gather | solution.py:23
  194.5 4.2 convolution_bitcast_fusion
  199.3 2.8 convolution_convert_fusion.1
  203.0 5.9 %fusion.26 = f32[512,512]{0,1:T(8,128)S(1)} fusion(bf16[4096,768]{1,0:T(8,128)(2,1)} %all-gather.5.cloned.1.call-done, bf16[1,512,4096]{2,1,0:T(8,128)(2,1)} %all-gather.9.cloned.1.call-done, f32[4096]{0:T(1024)S(1)} %copy-done.6, f32[512]{0:T(512)S(1)} %add_rsqrt_fusion), kind=kOutput, calls=%fused_computation.41 | convolution fusion | flops 2155872256 | bytes 9455616 | tf_op jit(solution)/shard_map/dot_general | solution.py:91
  214.5 2.5 fusion.40
  218.9 101.4 %while.22 = (s32[]{:T(128)}, bf16[2,512,128]{2,1,0:T(8,128)(2,1)S(1)}, f32[1,4,512]{2,1,0:T(4,128)S(1)}, f32[1,4,512]{2,1,0:T(4,128)S(1)}, f32[512,1,4,128]{3,0,...) while((s32[]{:T(128)}, ...), condition=%wide.region_8.9_spmd, body=%wide.region_4.8_spmd.sunk | while | flops 551334400 | bytes 18233720 | solution.py:127
  219.3 7.0 %collective-permute-done = bf16[2,512,128]{2,1,0:T(8,128)(2,1)S(1)} collective-permute-done((bf16[2,512,128]{2,1,0:T(8,128)(2,1)S(1)}, bf16[2,512,128]{2,1,0:T(8,128)(2,1)S(1)}, u32[]{:S(2)}, u32[]{:S(2)}) %collective-permute-start) | collective-permute-done | bytes 262176 | tf_op jit(solution)/shard_map/while/body/eval_jaxpr/ppermute | solution.py:29
  230.6 9.4 %collective-permute-done = bf16[2,512,128]{2,1,0:T(8,128)(2,1)S(1)} collective-permute-done((bf16[2,512,128]{2,1,0:T(8,128)(2,1)S(1)}, bf16[2,512,128]{2,1,0:T(8,128)(2,1)S(1)}, u32[]{:S(2)}, u32[]{:S(2)}) %collective-permute-start) | collective-permute-done | bytes 262176 | tf_op jit(solution)/shard_map/while/body/eval_jaxpr/ppermute | solution.py:29
  244.4 8.8 %collective-permute-done = bf16[2,512,128]{2,1,0:T(8,128)(2,1)S(1)} collective-permute-done((bf16[2,512,128]{2,1,0:T(8,128)(2,1)S(1)}, bf16[2,512,128]{2,1,0:T(8,128)(2,1)S(1)}, u32[]{:S(2)}, u32[]{:S(2)}) %collective-permute-start) | collective-permute-done | bytes 262176 | tf_op jit(solution)/shard_map/while/body/eval_jaxpr/ppermute | solution.py:29
  257.6 11.5 %collective-permute-done = bf16[2,512,128]{2,1,0:T(8,128)(2,1)S(1)} collective-permute-done((bf16[2,512,128]{2,1,0:T(8,128)(2,1)S(1)}, bf16[2,512,128]{2,1,0:T(8,128)(2,1)S(1)}, u32[]{:S(2)}, u32[]{:S(2)}) %collective-permute-start) | collective-permute-done | bytes 262176 | tf_op jit(solution)/shard_map/while/body/eval_jaxpr/ppermute | solution.py:29
  273.4 12.1 %collective-permute-done = bf16[2,512,128]{2,1,0:T(8,128)(2,1)S(1)} collective-permute-done((bf16[2,512,128]{2,1,0:T(8,128)(2,1)S(1)}, bf16[2,512,128]{2,1,0:T(8,128)(2,1)S(1)}, u32[]{:S(2)}, u32[]{:S(2)}) %collective-permute-start) | collective-permute-done | bytes 262176 | tf_op jit(solution)/shard_map/while/body/eval_jaxpr/ppermute | solution.py:29
  290.0 11.4 %collective-permute-done = bf16[2,512,128]{2,1,0:T(8,128)(2,1)S(1)} collective-permute-done((bf16[2,512,128]{2,1,0:T(8,128)(2,1)S(1)}, bf16[2,512,128]{2,1,0:T(8,128)(2,1)S(1)}, u32[]{:S(2)}, u32[]{:S(2)}) %collective-permute-start) | collective-permute-done | bytes 262176 | tf_op jit(solution)/shard_map/while/body/eval_jaxpr/ppermute | solution.py:29
  305.8 10.6 %collective-permute-done = bf16[2,512,128]{2,1,0:T(8,128)(2,1)S(1)} collective-permute-done((bf16[2,512,128]{2,1,0:T(8,128)(2,1)S(1)}, bf16[2,512,128]{2,1,0:T(8,128)(2,1)S(1)}, u32[]{:S(2)}, u32[]{:S(2)}) %collective-permute-start) | collective-permute-done | bytes 262176 | tf_op jit(solution)/shard_map/while/body/eval_jaxpr/ppermute | solution.py:29
  320.7 25.3 %all-gather.7.cloned.1.call-done = bf16[512,4096]{1,0:T(8,128)(2,1)} async-done(((bf16[512,128]{1,0:T(8,128)(2,1)}), bf16[512,4096]{1,0:T(8,128)(2,1)}) %all-gather.7.cloned.1.call-update) | async-done | bytes 4194320 | tf_op jit(solution)/shard_map/all_gather | solution.py:135
  346.1 6.5 %convolution_convert_fusion = bf16[512,4096]{1,0:T(8,128)(2,1)} fusion(bf16[512,512]{0,1:T(8,128)(2,1)S(1)} %bitcast.165, bf16[512,4096]{1,0:T(8,128)(2,1)} %all-gather.7.cloned.1.call-done), kind=kOutput, calls=%fused_computation.40 | convolution fusion | flops 2149580800 | bytes 8912896 | tf_op jit(solution)/shard_map/dot_general | solution.py:134
  352.6 69.7 %reduce-scatter.2.cloned.1.call-done = bf16[512,1024]{1,0:T(8,128)(2,1)} async-done(((bf16[512,4096]{1,0:T(8,128)(2,1)}), bf16[512,1024]{1,0:T(8,128)(2,1)}) %reduce-scatter.2.cloned.1.call-update) | async-done | bytes 1048592 | tf_op jit(solution)/shard_map/reduce_scatter | solution.py:137
  422.3 2.4 fusion.33
  424.7 9.2 %psum.35 = f32[]{:T(128)} all-reduce(f32[]{:T(128)} %fusion.33), channel_id=1, replica_groups=mesh['ctx_0'=4,'ctx_1'=2,'tp_0'=2,'tp_1'=2,'dp'=4] {'ctx_0'}, use_global_device_ids=true, to_apply=%region_11.12 | all-reduce | flops 1 | bytes 8 | tf_op jit(solution)/shard_map/psum | solution.py:34
  433.9 4.4 psum.36
  438.3 5.9 %psum.37 = f32[]{:T(128)} all-reduce(f32[]{:T(128)} %psum.36), channel_id=1, replica_groups=mesh['ctx_0'=4,'ctx_1'=2,'tp_0'=2,'tp_1'=2,'dp'=4] {'tp_0'}, use_global_device_ids=true, to_apply=%region_13.14 | all-reduce | flops 1 | bytes 8 | tf_op jit(solution)/shard_map/psum | solution.py:34
  444.2 7.9 %psum.38 = f32[]{:T(128)} all-reduce(f32[]{:T(128)} %psum.37), channel_id=1, replica_groups=mesh['ctx_0'=4,'ctx_1'=2,'tp_0'=2,'tp_1'=2,'dp'=4] {'tp_1'}, use_global_device_ids=true, to_apply=%region_14.15 | all-reduce | flops 1 | bytes 8 | tf_op jit(solution)/shard_map/psum | solution.py:34
  452.1 9.1 %psum.39 = f32[]{:T(128)} all-reduce(f32[]{:T(128)} %psum.38), channel_id=1, replica_groups=mesh['ctx_0'=4,'ctx_1'=2,'tp_0'=2,'tp_1'=2,'dp'=4] {'dp'}, use_global_device_ids=true, to_apply=%region_15.16 | all-reduce | flops 1 | bytes 8 | tf_op jit(solution)/shard_map/psum | solution.py:34
  (129 shorter events, 44.3 us)
Async XLA Ops:
  7.2 187.3 %copy-start.6 = (f32[4096]{0:T(1024)S(1)}, f32[4096]{0:T(1024)}, u32[]{:S(2)}) copy-start(f32[4096]{0:T(1024)} %param.12) | copy-start | bytes 49156
  7.2 44.6 %all-gather.9.cloned.1.call-start = ((), (), s32[]{:S(2)}) async-start(), calls=%async_computation.4 | async-start | bytes 5242880 | tf_op jit(solution)/shard_map/all_gather | solution.py:84
  7.9 186.6 %all-gather.5.cloned.1.call-start = ((), (), s32[]{:S(2)}) async-start(), calls=%async_computation.1 | async-start | bytes 6488064 | tf_op jit(solution)/shard_map/all_gather | solution.py:23
  9.6 336.5 %all-gather.7.cloned.1.call-start = ((), (), s32[]{:S(2)}) async-start(), calls=%async_computation.2 | async-start | bytes 4325376 | tf_op jit(solution)/shard_map/all_gather | solution.py:135
  10.4 412.0 %reduce-scatter.2.cloned.1.call-start = ((), (), s32[]{:S(2)}) async-start(), calls=%async_computation.3 | async-start | bytes 5242880 | tf_op jit(solution)/shard_map/reduce_scatter | solution.py:137
  194.5 4.8 %copy-start = (bf16[1,512,4096]{2,1,0:T(8,128)(2,1)S(1)}, bf16[1,512,4096]{2,1,0:T(8,128)(2,1)}, u32[]{:S(2)}) copy-start(bf16[1,512,4096]{2,1,0:T(8,128)(2,1)} %all-gather.9.cloned.1.call-done) | copy-start | bytes 12582916
  202.2 0.6 copy-start.3
  212.2 2.3 copy-start.4
  214.5 4.3 copy-start.5
  218.9 7.4 %collective-permute-start = (bf16[2,512,128]{2,1,0:T(8,128)(2,1)S(1)}, bf16[2,512,128]{2,1,0:T(8,128)(2,1)S(1)}, u32[]{:S(2)}, u32[]{:S(2)}) collective-permute-start(bf16[2,512,128]{2,1,0:T(8,128)(2,1)S(1)} %get-tuple-element.404), channel_id=1, source_target_pairs={{0,16},{16,32},{32,48},{48,64},{64,80},{80,96},{96,112},{112,0},{1... | collective-permute-start | bytes 786440 | tf_op jit(solution)/shard_map/while/body/eval_jaxpr/ppermute | solution.py:29
  230.2 9.9 %collective-permute-start = (bf16[2,512,128]{2,1,0:T(8,128)(2,1)S(1)}, bf16[2,512,128]{2,1,0:T(8,128)(2,1)S(1)}, u32[]{:S(2)}, u32[]{:S(2)}) collective-permute-start(bf16[2,512,128]{2,1,0:T(8,128)(2,1)S(1)} %get-tuple-element.404), channel_id=1, source_target_pairs={{0,16},{16,32},{32,48},{48,64},{64,80},{80,96},{96,112},{112,0},{1... | collective-permute-start | bytes 786440 | tf_op jit(solution)/shard_map/while/body/eval_jaxpr/ppermute | solution.py:29
  244.0 9.2 %collective-permute-start = (bf16[2,512,128]{2,1,0:T(8,128)(2,1)S(1)}, bf16[2,512,128]{2,1,0:T(8,128)(2,1)S(1)}, u32[]{:S(2)}, u32[]{:S(2)}) collective-permute-start(bf16[2,512,128]{2,1,0:T(8,128)(2,1)S(1)} %get-tuple-element.404), channel_id=1, source_target_pairs={{0,16},{16,32},{32,48},{48,64},{64,80},{80,96},{96,112},{112,0},{1... | collective-permute-start | bytes 786440 | tf_op jit(solution)/shard_map/while/body/eval_jaxpr/ppermute | solution.py:29
  257.2 11.9 %collective-permute-start = (bf16[2,512,128]{2,1,0:T(8,128)(2,1)S(1)}, bf16[2,512,128]{2,1,0:T(8,128)(2,1)S(1)}, u32[]{:S(2)}, u32[]{:S(2)}) collective-permute-start(bf16[2,512,128]{2,1,0:T(8,128)(2,1)S(1)} %get-tuple-element.404), channel_id=1, source_target_pairs={{0,16},{16,32},{32,48},{48,64},{64,80},{80,96},{96,112},{112,0},{1... | collective-permute-start | bytes 786440 | tf_op jit(solution)/shard_map/while/body/eval_jaxpr/ppermute | solution.py:29
  273.0 12.6 %collective-permute-start = (bf16[2,512,128]{2,1,0:T(8,128)(2,1)S(1)}, bf16[2,512,128]{2,1,0:T(8,128)(2,1)S(1)}, u32[]{:S(2)}, u32[]{:S(2)}) collective-permute-start(bf16[2,512,128]{2,1,0:T(8,128)(2,1)S(1)} %get-tuple-element.404), channel_id=1, source_target_pairs={{0,16},{16,32},{32,48},{48,64},{64,80},{80,96},{96,112},{112,0},{1... | collective-permute-start | bytes 786440 | tf_op jit(solution)/shard_map/while/body/eval_jaxpr/ppermute | solution.py:29
  289.5 11.9 %collective-permute-start = (bf16[2,512,128]{2,1,0:T(8,128)(2,1)S(1)}, bf16[2,512,128]{2,1,0:T(8,128)(2,1)S(1)}, u32[]{:S(2)}, u32[]{:S(2)}) collective-permute-start(bf16[2,512,128]{2,1,0:T(8,128)(2,1)S(1)} %get-tuple-element.404), channel_id=1, source_target_pairs={{0,16},{16,32},{32,48},{48,64},{64,80},{80,96},{96,112},{112,0},{1... | collective-permute-start | bytes 786440 | tf_op jit(solution)/shard_map/while/body/eval_jaxpr/ppermute | solution.py:29
  305.3 11.0 %collective-permute-start = (bf16[2,512,128]{2,1,0:T(8,128)(2,1)S(1)}, bf16[2,512,128]{2,1,0:T(8,128)(2,1)S(1)}, u32[]{:S(2)}, u32[]{:S(2)}) collective-permute-start(bf16[2,512,128]{2,1,0:T(8,128)(2,1)S(1)} %get-tuple-element.404), channel_id=1, source_target_pairs={{0,16},{16,32},{32,48},{48,64},{64,80},{80,96},{96,112},{112,0},{1... | collective-permute-start | bytes 786440 | tf_op jit(solution)/shard_map/while/body/eval_jaxpr/ppermute | solution.py:29
  352.6 69.8 %copy-start.1 = (bf16[1,512,1024]{2,1,0:T(8,128)(2,1)S(1)}, bf16[1,512,1024]{2,1,0:T(8,128)(2,1)}, u32[]{:S(2)}) copy-start(bf16[1,512,1024]{2,1,0:T(8,128)(2,1)} %param.10) | copy-start | bytes 3145732
  352.6 69.8 %copy-start.2 = (bf16[1,512,1024]{2,1,0:T(8,128)(2,1)S(1)}, bf16[1,512,1024]{2,1,0:T(8,128)(2,1)}, u32[]{:S(2)}) copy-start(bf16[1,512,1024]{2,1,0:T(8,128)(2,1)} %param.11) | copy-start | bytes 3145732
Sparse Core Ops, SparseCore 0:
  9.7 42.0 all-gather.8
  54.0 140.4 all-gather.4
  196.1 149.9 all-gather.6
  352.7 69.5 reduce-scatter.1
where the time goes:
time: 471 us; the launch traced here: 470 us
  waiting for transfers between devices  346 us (73%)
  matrix products  42.7 us (9%)
  blocking collectives  36.5 us (8%)
  other arithmetic  22.4 us (5%)
  between operations  15.7 us (3%)
    all_gather x1, waiting for transfers between devices, side_by_side(): whole = lax.all_gather(both, axis, axis=dim, tiled=True)  140 us
    ppermute x7, waiting for transfers between devices, shifted(): lax.ppermute(value, axis, [(i, (i + by) % peers) for i in range(peers)])  70.8 us
    reduce_scatter x1, waiting for transfers between devices, on_device(): lax.psum_scatter(terms.astype(jnp.bfloat16), TP, scatter_dimension=1, til...  69.7 us
    all_gather x1, waiting for transfers between devices, on_device(): whole = lax.all_gather(local, TP, axis=1, tiled=True)  39.4 us
    psum x5, blocking collectives, by_axis(): value = lax.psum(value, axis)  36.5 us
    all_gather x1, waiting for transfers between devices, on_device(): lax.all_gather(w_out, CTX_DP, axis=1, tiled=True)  25.3 us
    dot_general x8, matrix products, attend(): jnp.einsum('cgqk,kcd->qcgd', weights.astype(jnp.bfloat16), pair[1], prefe...  15.8 us
    dot_general x3, matrix products, on_device(): jnp.dot(normed, piece, preferred_element_type=jnp.float32)  13 us
  transfers between devices with their start and end apart: 11, of which 11 were waited for; matrix products, arithmetic and copies ran while one was open for 13% of the time, Pallas kernels for 0%

commit v1 on v0

--- a/solution.py
+++ b/solution.py
@@ -1,17 +1,20 @@
+import types
+
 import jax
 import jax.numpy as jnp
 from jax import lax
-from jax.sharding import Mesh
+from jax.experimental import pallas as pl
+from jax.experimental.pallas import tpu as pltpu
 from jax.sharding import PartitionSpec as P
 
 MODEL_WIDTH = 4096
 QUERY_HEADS = 16
 KEY_VALUE_HEADS = 4
 HEAD_SIZE = 128
-TP = ("tp_0", "tp_1")
-CTX_DP = ("ctx_0", "ctx_1", "dp")
-CTX = ("ctx_0", "ctx_1")
-CTX_TP_DP = ("ctx_0", "ctx_1", "tp_0", "tp_1", "dp")
+TP = "tp"
+CTX_DP = ("ctx", "dp")
+CTX = "ctx"
+CTX_TP_DP = ("ctx", "tp", "dp")
 
 
 rope_base = 500000.0
@@ -54,6 +57,253 @@
     return jnp.concatenate(
         [first * cosine - second * sine, second * cosine + first * sine], axis=-1
     )
+
+
+MESH = pl.DeviceIdType.MESH
+SIDES = (1, -1)
+
+
+def here():
+    c, t, d = lax.axis_index("ctx"), lax.axis_index("tp"), lax.axis_index("dp")
+    return c, t, d
+
+
+class Net:
+    def __init__(self, send_sems, recv_sems):
+        self.send_sems, self.recv_sems = send_sems, recv_sems
+        self.started = []
+
+    def copy(self, k, src, dst, dev):
+        c, t, d = dev
+        return pltpu.make_async_remote_copy(
+            src_ref=src,
+            dst_ref=dst,
+            send_sem=self.send_sems.at[k],
+            recv_sem=self.recv_sems.at[k],
+            device_id=(c, t, d),
+            device_id_type=MESH,
+        )
+
+    def send(self, ref, dev, dst=None):
+        k = len(self.started)
+        copy = self.copy(k, ref, ref if dst is None else dst, dev)
+        copy.start()
+        self.started.append((copy, dev))
+        return k
+
+    def recv(self, k, ref):
+        self.copy(k, ref, ref, self.started[k][1]).wait_recv()
+
+    def finish(self):
+        for copy, _ in self.started:
+            copy.wait_send()
+
+
+def places():
+    c, t, d = here()
+    z, xl = c // 2, c % 2
+    c1 = c + 1 - 2 * xl
+    t1 = t + 1 - 2 * (t % 2)
+    t2 = (t + 2) % 4
+    t3 = (t1 + 2) % 4
+    return types.SimpleNamespace(
+        c=c, t=t, d=d, z=z, xl=xl, xo=1 - xl, c1=c1, t1=t1, t2=t2, t3=t3,
+        P=(c1, t, d), Q=(c1, t2, d), C=(c, t1, d), R=(c, t2, d), D=(c, t3, d),
+        Y={s: (c, t, (d + s) % 4) for s in SIDES},
+        Z={s: ((c + 2 * s) % 8, t, d) for s in SIDES},
+        yo={s: (d - s) % 4 for s in SIDES},
+        zo={s: (z - s) % 4 for s in SIDES},
+        y2=(d + 2) % 4, z2=(z + 2) % 4,
+    )
+
+
+def greet(m):
+    barrier = pltpu.get_barrier_semaphore()
+    others = [m.P, m.Q, m.C, m.R, m.D, m.Y[1], m.Y[-1], m.Z[1], m.Z[-1]]
+    for dev in others:
+        pl.semaphore_signal(barrier, inc=1, device_id=dev, device_id_type=MESH)
+    pl.semaphore_wait(barrier, len(others))
+
+
+def front_kernel(hid, wq, wk, wv, gain, cos, sin, q_out, kv_out, H, N, RH, W, acc, ssem, rsem, lsem):
+    m = places()
+    net = Net(ssem, rsem)
+    c, t, d = m.c, m.t, m.d
+    local = [
+        pltpu.make_async_copy(wq, W.at[c, d, :, pl.ds(0, 512)], lsem.at[0]),
+        pltpu.make_async_copy(wk, W.at[c, d, :, pl.ds(512, 128)], lsem.at[1]),
+        pltpu.make_async_copy(wv, W.at[c, d, :, pl.ds(640, 128)], lsem.at[2]),
+        pltpu.make_async_copy(hid.at[0], H.at[t], lsem.at[3]),
+    ]
+    for cp in local:
+        cp.start()
+    greet(m)
+    for cp in local:
+        cp.wait()
+
+    def pair(z):
+        return pl.ds(2 * z, 2)
+
+    qa = {1: pl.ds(0, 32), -1: pl.ds(32, 32)}
+    qb = {1: pl.ds(64, 32), -1: pl.ds(96, 32)}
+    ha, hb = pl.ds(0, 64), pl.ds(64, 64)
+    parts = 2
+    rows = 256 // parts
+
+    kX = net.send(W.at[c, d], m.P)
+    kY1 = {s: net.send(W.at[c, d], m.Y[s]) for s in SIDES}
+    kZ1 = {s: net.send(W.at[c, d], m.Z[s]) for s in SIDES}
+    kH0 = [net.send(H.at[t, pl.ds(i * rows, rows)], m.P, RH.at[0, pl.ds(i * rows, rows)]) for i in range(parts)]
+    kH1 = [net.send(H.at[t, pl.ds(256 + i * rows, rows)], m.Q, RH.at[1, pl.ds(i * rows, rows)]) for i in range(parts)]
+    kC = net.send(H.at[t], m.C)
+
+    net.recv(kX, W.at[m.c1, d])
+    kY2 = {s: net.send(W.at[m.c1, d], m.Y[s]) for s in SIDES}
+    kZ2 = {s: net.send(W.at[m.c1, d], m.Z[s]) for s in SIDES}
+
+    fY, fZ, kY3, kZ3, kY4, kZ4 = {}, {}, {}, {}, {}, {}
+    for s in SIDES:
+        net.recv(kY1[s], W.at[c, m.yo[s]])
+        net.recv(kZ1[s], W.at[2 * m.zo[s] + m.xl, d])
+    for s in SIDES:
+        net.recv(kY2[s], W.at[m.c1, m.yo[s]])
+        kY3[s] = net.send(W.at[pair(m.z), m.yo[s], qa[s]], m.Y[s])
+        net.recv(kZ2[s], W.at[2 * m.zo[s] + m.xo, d])
+        kZ3[s] = net.send(W.at[pair(m.zo[s]), d, qb[s]], m.Z[s])
+    for s in SIDES:
+        for r in SIDES:
+            kZ4[s, r] = net.send(W.at[pair(m.z), m.yo[s], ha], m.Z[r])
+            kY4[s, r] = net.send(W.at[pair(m.zo[s]), d, hb], m.Y[r])
+
+    def relay(i):
+        net.recv(kH0[i], RH.at[0, pl.ds(i * rows, rows)])
+        a = net.send(RH.at[0, pl.ds(i * rows, rows)], m.Q, H.at[t, pl.ds(i * rows, rows)])
+        net.recv(kH1[i], RH.at[1, pl.ds(i * rows, rows)])
+        b = net.send(RH.at[1, pl.ds(i * rows, rows)], m.P, H.at[m.t2, pl.ds(256 + i * rows, rows)])
+        return a, b
+
+    def landed(k):
+        out = []
+        for i in range(parts):
+            for k_, lo in ((k[i][0], i * rows), (k[i][1], 256 + i * rows)):
+                net.recv(k_, H.at[m.t2, pl.ds(lo, rows)])
+                out.append((net.send(H.at[m.t2, pl.ds(lo, rows)], m.C), lo))
+        return out
+
+    kF = [relay(0)]
+    kY6, kZ6 = {}, {}
+    for s in SIDES:
+        net.recv(kY3[s], W.at[pair(m.z), m.y2, qa[s]])
+        net.recv(kZ3[s], W.at[pair(m.z2), d, qb[s]])
+    for r in SIDES:
+        kZ6[r] = net.send(W.at[pair(m.z), m.y2, ha], m.Z[r])
+        kY6[r] = net.send(W.at[pair(m.z2), d, hb], m.Y[r])
+    for s in SIDES:
+        fZ[s, "own"] = net.send(W.at[pair(m.zo[s]), d, qa[s]], m.Z[s])
+        fY[s, "own"] = net.send(W.at[pair(m.z), m.yo[s], qb[s]], m.Y[s])
+    kF += [relay(i) for i in range(1, parts)]
+    for s in SIDES:
+        for r in SIDES:
+            net.recv(kZ4[s, r], W.at[pair(m.zo[r]), m.yo[s], ha])
+            fZ[r, s] = net.send(W.at[pair(m.zo[r]), m.yo[s], qa[r]], m.Z[r])
+            net.recv(kY4[s, r], W.at[pair(m.zo[s]), m.yo[r], hb])
+            fY[r, s] = net.send(W.at[pair(m.zo[s]), m.yo[r], qb[r]], m.Y[r])
+    for r in SIDES:
+        net.recv(kZ6[r], W.at[pair(m.zo[r]), m.y2, ha])
+        fZ[r, "far"] = net.send(W.at[pair(m.zo[r]), m.y2, qa[r]], m.Z[r])
+        net.recv(kY6[r], W.at[pair(m.z2), m.yo[r], hb])
+        fY[r, "far"] = net.send(W.at[pair(m.z2), m.yo[r], qb[r]], m.Y[r])
+    far = landed(kF)
+    net.recv(kC, H.at[m.t1])
+    for k, lo in far:
+        net.recv(k, H.at[m.t3, pl.ds(lo, rows)])
+
+    step = 64
+
+    def norm(i, carry):
+        at = pl.ds(pl.multiple_of(i * step, step), step)
+        total = jnp.zeros((step, 1), jnp.float32)
+        for b in range(4):
+            x = H[b, at, :].astype(jnp.float32)
+            total = total + jnp.sum(x * x, axis=1, keepdims=True)
+        scale = lax.rsqrt(total * (1.0 / MODEL_WIDTH) + 1e-05)
+        for b in range(4):
+            x = H[b, at, :].astype(jnp.float32)
+            g = gain[:, b * 1024 : (b + 1) * 1024]
+            N[b, at, :] = (x * scale * g).astype(jnp.bfloat16)
+        return carry
+
+    lax.fori_loop(0, 512 // step, norm, 0)
+
+    def chunk(z, first):
+        for n in range(3):
+            cols = pl.ds(n * 256, 256)
+            w = W[pair(z), :, :, cols].reshape(1024, 256)
+            part = jnp.dot(N[z], w, preferred_element_type=jnp.float32)
+            if first:
+                acc[:, cols] = part
+            else:
+                acc[:, cols] += part
+
+    for r in SIDES:
+        net.recv(fY[r, "own"], W.at[pair(m.z), m.y2, qb[r]])
+    chunk(m.z, True)
+    for s in SIDES:
+        for r in SIDES:
+            net.recv(fY[r, s], W.at[pair(m.zo[s]), m.y2, qb[r]])
+    for s in SIDES:
+        chunk(m.zo[s], False)
+    for r in SIDES:
+        net.recv(fZ[r, "own"], W.at[pair(m.z2), d, qa[r]])
+        for s in SIDES:
+            net.recv(fZ[r, s], W.at[pair(m.z2), m.yo[s], qa[r]])
+        net.recv(fZ[r, "far"], W.at[pair(m.z2), m.y2, qa[r]])
+        net.recv(fY[r, "far"], W.at[pair(m.z2), m.y2, qb[r]])
+    chunk(m.z2, False)
+
+    def rope(i, carry):
+        at = pl.ds(pl.multiple_of(i * step, step), step)
+        co, si = cos[at, :], sin[at, :]
+        for h in range(5):
+            x = acc[at, h * 128 : (h + 1) * 128]
+            y = (x * co + pltpu.roll(x, 64, 1) * si).astype(jnp.bfloat16)
+            if h < 4:
+                q_out[h, at, :] = y
+            else:
+                kv_out[0, at, :] = y
+        kv_out[1, at, :] = acc[at, 640:768].astype(jnp.bfloat16)
+        return carry
+
+    lax.fori_loop(0, 512 // step, rope, 0)
+    net.finish()
+
+
+def front(hidden, wq, wk, wv, gain, cos, sin):
+    any_spec = pl.BlockSpec(memory_space=pl.ANY)
+    vmem = pl.BlockSpec(memory_space=pltpu.VMEM)
+    return pl.pallas_call(
+        front_kernel,
+        out_shape=(
+            jax.ShapeDtypeStruct((4, 512, 128), jnp.bfloat16),
+            jax.ShapeDtypeStruct((2, 512, 128), jnp.bfloat16),
+        ),
+        in_specs=[any_spec] * 4 + [vmem] * 3,
+        out_specs=(vmem, vmem),
+        scratch_shapes=[
+            pltpu.VMEM((4, 512, 1024), jnp.bfloat16),
+            pltpu.VMEM((4, 512, 1024), jnp.bfloat16),
+            pltpu.VMEM((2, 256, 1024), jnp.bfloat16),
+            pltpu.VMEM((8, 4, 128, 768), jnp.bfloat16),
+            pltpu.VMEM((512, 768), jnp.float32),
+            pltpu.SemaphoreType.DMA((64,)),
+            pltpu.SemaphoreType.DMA((64,)),
+            pltpu.SemaphoreType.DMA((4,)),
+        ],
+        compiler_params=pltpu.CompilerParams(
+            collective_id=0, has_side_effects=True, vmem_limit_bytes=60 * 1024 * 1024
+        ),
+        name="front",
+    )(hidden, wq, wk, wv, gain, cos, sin)
 
 
 def attend(state, query_rows, qpos, piece, kpos):
@@ -81,30 +331,15 @@
     rows = hidden.shape[1]
     half = rows // 2
     local = hidden[0]
-    whole = lax.all_gather(local, TP, axis=1, tiled=True)
-    wide = whole.astype(jnp.float32)
-    normed = (
-        wide * lax.rsqrt(jnp.mean(wide * wide, axis=1, keepdims=True) + 1e-05) * gain[None, :]
-    ).astype(jnp.bfloat16)
-    pieces = side_by_side((w_query, w_key, value_matrix), CTX_DP, 0, 1)
-    query_rows, key, value_rows = tuple(
-        (jnp.dot(normed, piece, preferred_element_type=jnp.float32) for piece in pieces)
-    )
     shard = lax.axis_index(CTX)
     qpos = positions(block_order, shard * rows, rows, half)
     local_heads = w_key.shape[1] // HEAD_SIZE
     query_group = QUERY_HEADS // KEY_VALUE_HEADS
-    query_rows = (
-        apply_rotary(query_rows.reshape(rows, local_heads * query_group, HEAD_SIZE), qpos)
-        .astype(jnp.bfloat16)
-        .reshape(rows, local_heads, query_group, HEAD_SIZE)
-    )
-    key = (
-        apply_rotary(key.reshape(rows, local_heads, HEAD_SIZE), qpos)
-        .astype(jnp.bfloat16)
-        .reshape(rows, local_heads * HEAD_SIZE)
-    )
-    pair = jnp.stack([key, value_rows.astype(jnp.bfloat16)])
+    angles = qpos.astype(jnp.float32)[:, None] * (rope_base ** (-(jnp.arange(64, dtype=jnp.float32) * 2.0) / 128))[None, :]
+    co, si = jnp.cos(angles), jnp.sin(angles)
+    co, si = jnp.concatenate([co, co], 1), jnp.concatenate([-si, si], 1)
+    q, pair = front(hidden, w_query, w_key, value_matrix, gain[None, :], co, si)
+    query_rows = jnp.transpose(q, (1, 0, 2)).reshape(rows, local_heads, query_group, HEAD_SIZE)
     state = (
         jnp.full((local_heads, query_group, rows), -1e30, jnp.float32),
         jnp.zeros((local_heads, query_group, rows), jnp.float32),
@@ -136,15 +371,12 @@
     )
     summed = lax.psum_scatter(terms.astype(jnp.bfloat16), TP, scatter_dimension=1, tiled=True)
     resid = local.astype(jnp.float32) + summed.astype(jnp.float32) - target[0].astype(jnp.float32)
-    squares = by_axis(jnp.sum(resid * resid), CTX_TP_DP)
+    squares = lax.psum(jnp.sum(resid * resid), CTX_TP_DP)
     loss = squares / (lax.axis_size("dp") * lax.axis_size(CTX) * rows * MODEL_WIDTH)
     return (summed[None], loss)
 
 
 def solution(mesh):
-    split = Mesh(
-        mesh.devices.reshape(4, 2, 2, 2, mesh.shape["dp"]), ("ctx_0", "ctx_1", "tp_0", "tp_1", "dp")
-    )
     placed = (
         P("dp", CTX, TP),
         P("dp", CTX, TP),
@@ -156,5 +388,5 @@
         P(),
     )
     return jax.shard_map(
-        on_device, mesh=split, in_specs=placed, out_specs=(P("dp", CTX, TP), P()), check_vma=False
-    )
+        on_device, mesh=mesh, in_specs=placed, out_specs=(P("dp", CTX, TP), P()), check_vma=False
+    )

time: 471 us -> 312 us (0.66)
  waiting for transfers between devices: 346 us -> 124 us
  Pallas kernels: 0 us -> 59.6 us
  blocking collectives: 36.5 us -> 65.1 us
  matrix products: 42.7 us -> 28.2 us
  other arithmetic: 22.4 us -> 16.3 us
    all_gather x2 -> x0, waiting for transfers between devices: 179 us -> none  [the longest x1 140 us: side_by_side(): whole = lax.all_gather(both, axis, axis=dim, tiled=True)]
    pallas_call x0 -> x1, Pallas kernels: none -> 59.6 us  [front(): pl.pallas_call(front_kernel, out_shape=(jax.ShapeDtypeStruct((4, 512, 128...]
    psum x5 -> x1, blocking collectives: 36.5 us -> 65.1 us  [on_device(): squares = lax.psum(jnp.sum(resid * resid), CTX_TP_DP)]
    all_gather x1, waiting for transfers between devices: 25.3 us -> 0.02 us  [on_device(): lax.all_gather(w_out, CTX_DP, axis=1, tiled=True)]
    dot_general x3 -> x0, matrix products: 13 us -> none  [on_device(): jnp.dot(normed, piece, preferred_element_type=jnp.float32)]
    reduce_scatter x1, waiting for transfers between devices: 69.7 us -> 58.9 us  [on_device(): lax.psum_scatter(terms.astype(jnp.bfloat16), TP, scatter_dimension=1, til...]
    ppermute x7, waiting for transfers between devices: 70.8 us -> 64.5 us  [shifted(): lax.ppermute(value, axis, [(i, (i + by) % peers) for i in range(peers)])]
  transfers between devices with their start and end apart: 11 -> 9, of which waited for: 11 -> 8; matrix products, arithmetic and copies ran while one was open for 13% -> 12% of each run, Pallas kernels for 0% -> 19%
where the time goes in v1:
time: 312 us; the launch traced here: 311 us
  waiting for transfers between devices  124 us (40%)
  blocking collectives  65.1 us (21%)
  Pallas kernels  59.6 us (19%)
  matrix products  28.2 us (9%)
  other arithmetic  16.3 us (5%)
  between operations  15.9 us (5%)
    psum x1, blocking collectives, on_device(): squares = lax.psum(jnp.sum(resid * resid), CTX_TP_DP)  65.1 us
    ppermute x7, waiting for transfers between devices, shifted(): lax.ppermute(value, axis, [(i, (i + by) % peers) for i in range(peers)])  64.5 us
    pallas_call x1, Pallas kernels, front(): pl.pallas_call(front_kernel, out_shape=(jax.ShapeDtypeStruct((4, 512, 128...  59.6 us
    reduce_scatter x1, waiting for transfers between devices, on_device(): lax.psum_scatter(terms.astype(jnp.bfloat16), TP, scatter_dimension=1, til...  58.9 us
    dot_general x8, matrix products, attend(): jnp.einsum('cgqk,kcd->qcgd', weights.astype(jnp.bfloat16), pair[1], prefe...  14.7 us
    reduce_sum x8, other arithmetic, attend(): total = total * factor + jnp.sum(weights, axis=-1)  8.34 us
    dot_general x8, matrix products, attend(): jnp.einsum('qcgd,kcd->cgqk', query_rows, pair[0], preferred_element_type=...  6.98 us
    dot_general x1, matrix products, on_device(): jnp.dot(attn, lax.all_gather(w_out, CTX_DP, axis=1, tiled=True), preferre...  6.53 us
  transfers between devices with their start and end apart: 9, of which 8 were waited for; matrix products, arithmetic and copies ran while one was open for 12% of the time, Pallas kernels for 19%

profile of v1, /device:TPU:1, one launch (start us, length us, event | category | flops | bytes accessed | tf_op | source)
XLA Modules:
  0.0 311.5 jit_solution(17996505763290731042)
XLA Ops:
  10.9 59.6 %front.1 = (bf16[4,512,128]{2,1,0:T(8,128)(2,1)S(1)}, bf16[2,512,128]{2,1,0:T(8,128)(2,1)S(1)}) custom-call(bf16[1,512,1024]{2,1,0:T(8,128)(2,1)} %hid.1, bf16[128,512]{1,0:T(8,128)(2,1)} %wq.1, bf16[128,128]{1,0:T(8,128)(2,1)} %wk.1, bf16[128,128]{1,0:T(8,128)(2,1)} %wv.1, f32[1,4096]{1,0:T(1,128)} %bitcast.161, f32[512,128]{1,0:T(8,128)} %get-tuple-element.325.cos, ...), custom_call_target="tpu_custom_call" | custom-call | tf_op jit(solution)/shard_map/front/pallas_call | solution.py:284
  71.4 1.1 fusion.25
  72.5 1.3 fusion.35
  74.2 95.3 %while.22 = (s32[]{:T(128)}, bf16[2,512,128]{2,1,0:T(8,128)(2,1)S(1)}, f32[1,4,512]{2,1,0:T(4,128)S(1)}, f32[1,4,512]{2,1,0:T(4,128)S(1)}, f32[512,1,4,128]{3,0,...) while((s32[]{:T(128)}, ...), condition=%wide.region_7.8_spmd, body=%wide.region_3.7_spmd.sunk | while | flops 551334400 | bytes 18233720 | solution.py:362
  74.6 11.0 %collective-permute-done = bf16[2,512,128]{2,1,0:T(8,128)(2,1)S(1)} collective-permute-done((bf16[2,512,128]{2,1,0:T(8,128)(2,1)S(1)}, bf16[2,512,128]{2,1,0:T(8,128)(2,1)S(1)}, u32[]{:S(2)}, u32[]{:S(2)}) %collective-permute-start) | collective-permute-done | bytes 262176 | tf_op jit(solution)/shard_map/while/body/eval_jaxpr/ppermute | solution.py:32
  86.5 1.0 fusion.68
  87.7 1.9 fusion.69
  90.0 10.8 %collective-permute-done = bf16[2,512,128]{2,1,0:T(8,128)(2,1)S(1)} collective-permute-done((bf16[2,512,128]{2,1,0:T(8,128)(2,1)S(1)}, bf16[2,512,128]{2,1,0:T(8,128)(2,1)S(1)}, u32[]{:S(2)}, u32[]{:S(2)}) %collective-permute-start) | collective-permute-done | bytes 262176 | tf_op jit(solution)/shard_map/while/body/eval_jaxpr/ppermute | solution.py:32
  102.8 1.9 fusion.69
  105.2 8.2 %collective-permute-done = bf16[2,512,128]{2,1,0:T(8,128)(2,1)S(1)} collective-permute-done((bf16[2,512,128]{2,1,0:T(8,128)(2,1)S(1)}, bf16[2,512,128]{2,1,0:T(8,128)(2,1)S(1)}, u32[]{:S(2)}, u32[]{:S(2)}) %collective-permute-start) | collective-permute-done | bytes 262176 | tf_op jit(solution)/shard_map/while/body/eval_jaxpr/ppermute | solution.py:32
  115.4 1.9 fusion.69
  117.8 9.1 %collective-permute-done = bf16[2,512,128]{2,1,0:T(8,128)(2,1)S(1)} collective-permute-done((bf16[2,512,128]{2,1,0:T(8,128)(2,1)S(1)}, bf16[2,512,128]{2,1,0:T(8,128)(2,1)S(1)}, u32[]{:S(2)}, u32[]{:S(2)}) %collective-permute-start) | collective-permute-done | bytes 262176 | tf_op jit(solution)/shard_map/while/body/eval_jaxpr/ppermute | solution.py:32
  128.8 1.9 fusion.69
  131.2 8.4 %collective-permute-done = bf16[2,512,128]{2,1,0:T(8,128)(2,1)S(1)} collective-permute-done((bf16[2,512,128]{2,1,0:T(8,128)(2,1)S(1)}, bf16[2,512,128]{2,1,0:T(8,128)(2,1)S(1)}, u32[]{:S(2)}, u32[]{:S(2)}) %collective-permute-start) | collective-permute-done | bytes 262176 | tf_op jit(solution)/shard_map/while/body/eval_jaxpr/ppermute | solution.py:32
  141.7 1.9 fusion.69
  144.0 7.5 %collective-permute-done = bf16[2,512,128]{2,1,0:T(8,128)(2,1)S(1)} collective-permute-done((bf16[2,512,128]{2,1,0:T(8,128)(2,1)S(1)}, bf16[2,512,128]{2,1,0:T(8,128)(2,1)S(1)}, u32[]{:S(2)}, u32[]{:S(2)}) %collective-permute-start) | collective-permute-done | bytes 262176 | tf_op jit(solution)/shard_map/while/body/eval_jaxpr/ppermute | solution.py:32
  152.5 1.0 fusion.68
  153.6 1.9 fusion.69
  155.9 9.4 %collective-permute-done = bf16[2,512,128]{2,1,0:T(8,128)(2,1)S(1)} collective-permute-done((bf16[2,512,128]{2,1,0:T(8,128)(2,1)S(1)}, bf16[2,512,128]{2,1,0:T(8,128)(2,1)S(1)}, u32[]{:S(2)}, u32[]{:S(2)}) %collective-permute-start) | collective-permute-done | bytes 262176 | tf_op jit(solution)/shard_map/while/body/eval_jaxpr/ppermute | solution.py:32
  167.3 1.9 fusion.69
  169.9 6.5 %convolution_convert_fusion = bf16[512,4096]{1,0:T(8,128)(2,1)} fusion(bf16[512,512]{0,1:T(8,128)(2,1)S(1)} %bitcast.158, bf16[512,4096]{1,0:T(8,128)(2,1)} %all-gather.2.cloned.1.call-done), kind=kOutput, calls=%fused_computation.35 | convolution fusion | flops 2149580800 | bytes 8912896 | tf_op jit(solution)/shard_map/dot_general | solution.py:369
  176.5 58.9 %reduce-scatter.2.cloned.1.call-done = bf16[512,1024]{1,0:T(8,128)(2,1)} async-done(((bf16[512,4096]{1,0:T(8,128)(2,1)}), bf16[512,1024]{1,0:T(8,128)(2,1)}) %reduce-scatter.2.cloned.1.call-update) | async-done | bytes 1048592 | tf_op jit(solution)/shard_map/reduce_scatter | solution.py:372
  235.4 2.4 fusion.28
  237.8 65.1 %psum.7 = f32[]{:T(128)} all-reduce(f32[]{:T(128)} %fusion.28), channel_id=1, replica_groups=mesh['ctx'=8,'tp'=4,'dp'=4] {'ctx','tp','dp'}, use_global_device_ids=true, to_apply=%region_10.11 | all-reduce | flops 1 | bytes 8 | tf_op jit(solution)/shard_map/psum | solution.py:374
  (99 shorter events, 19.9 us)
Async XLA Ops:
  7.2 162.8 %all-gather.2.cloned.1.call-start = ((), (), s32[]{:S(2)}) async-start(), calls=%async_computation.1 | async-start | bytes 4325376 | tf_op jit(solution)/shard_map/all_gather | solution.py:370
  7.9 227.5 %reduce-scatter.2.cloned.1.call-start = ((), (), s32[]{:S(2)}) async-start(), calls=%async_computation.2 | async-start | bytes 5242880 | tf_op jit(solution)/shard_map/reduce_scatter | solution.py:372
  72.5 1.7 copy-start.2
  74.2 11.5 %collective-permute-start = (bf16[2,512,128]{2,1,0:T(8,128)(2,1)S(1)}, bf16[2,512,128]{2,1,0:T(8,128)(2,1)S(1)}, u32[]{:S(2)}, u32[]{:S(2)}) collective-permute-start(bf16[2,512,128]{2,1,0:T(8,128)(2,1)S(1)} %get-tuple-element.405), channel_id=1, source_target_pairs={{0,16},{16,32},{32,48},{48,64},{64,80},{80,96},{96,112},{112,0},{1... | collective-permute-start | bytes 786440 | tf_op jit(solution)/shard_map/while/body/eval_jaxpr/ppermute | solution.py:32
  89.6 11.2 %collective-permute-start = (bf16[2,512,128]{2,1,0:T(8,128)(2,1)S(1)}, bf16[2,512,128]{2,1,0:T(8,128)(2,1)S(1)}, u32[]{:S(2)}, u32[]{:S(2)}) collective-permute-start(bf16[2,512,128]{2,1,0:T(8,128)(2,1)S(1)} %get-tuple-element.405), channel_id=1, source_target_pairs={{0,16},{16,32},{32,48},{48,64},{64,80},{80,96},{96,112},{112,0},{1... | collective-permute-start | bytes 786440 | tf_op jit(solution)/shard_map/while/body/eval_jaxpr/ppermute | solution.py:32
  104.7 8.7 %collective-permute-start = (bf16[2,512,128]{2,1,0:T(8,128)(2,1)S(1)}, bf16[2,512,128]{2,1,0:T(8,128)(2,1)S(1)}, u32[]{:S(2)}, u32[]{:S(2)}) collective-permute-start(bf16[2,512,128]{2,1,0:T(8,128)(2,1)S(1)} %get-tuple-element.405), channel_id=1, source_target_pairs={{0,16},{16,32},{32,48},{48,64},{64,80},{80,96},{96,112},{112,0},{1... | collective-permute-start | bytes 786440 | tf_op jit(solution)/shard_map/while/body/eval_jaxpr/ppermute | solution.py:32
  117.3 9.5 %collective-permute-start = (bf16[2,512,128]{2,1,0:T(8,128)(2,1)S(1)}, bf16[2,512,128]{2,1,0:T(8,128)(2,1)S(1)}, u32[]{:S(2)}, u32[]{:S(2)}) collective-permute-start(bf16[2,512,128]{2,1,0:T(8,128)(2,1)S(1)} %get-tuple-element.405), channel_id=1, source_target_pairs={{0,16},{16,32},{32,48},{48,64},{64,80},{80,96},{96,112},{112,0},{1... | collective-permute-start | bytes 786440 | tf_op jit(solution)/shard_map/while/body/eval_jaxpr/ppermute | solution.py:32
  130.8 8.9 %collective-permute-start = (bf16[2,512,128]{2,1,0:T(8,128)(2,1)S(1)}, bf16[2,512,128]{2,1,0:T(8,128)(2,1)S(1)}, u32[]{:S(2)}, u32[]{:S(2)}) collective-permute-start(bf16[2,512,128]{2,1,0:T(8,128)(2,1)S(1)} %get-tuple-element.405), channel_id=1, source_target_pairs={{0,16},{16,32},{32,48},{48,64},{64,80},{80,96},{96,112},{112,0},{1... | collective-permute-start | bytes 786440 | tf_op jit(solution)/shard_map/while/body/eval_jaxpr/ppermute | solution.py:32
  143.6 8.0 %collective-permute-start = (bf16[2,512,128]{2,1,0:T(8,128)(2,1)S(1)}, bf16[2,512,128]{2,1,0:T(8,128)(2,1)S(1)}, u32[]{:S(2)}, u32[]{:S(2)}) collective-permute-start(bf16[2,512,128]{2,1,0:T(8,128)(2,1)S(1)} %get-tuple-element.405), channel_id=1, source_target_pairs={{0,16},{16,32},{32,48},{48,64},{64,80},{80,96},{96,112},{112,0},{1... | collective-permute-start | bytes 786440 | tf_op jit(solution)/shard_map/while/body/eval_jaxpr/ppermute | solution.py:32
  155.5 9.8 %collective-permute-start = (bf16[2,512,128]{2,1,0:T(8,128)(2,1)S(1)}, bf16[2,512,128]{2,1,0:T(8,128)(2,1)S(1)}, u32[]{:S(2)}, u32[]{:S(2)}) collective-permute-start(bf16[2,512,128]{2,1,0:T(8,128)(2,1)S(1)} %get-tuple-element.405), channel_id=1, source_target_pairs={{0,16},{16,32},{32,48},{48,64},{64,80},{80,96},{96,112},{112,0},{1... | collective-permute-start | bytes 786440 | tf_op jit(solution)/shard_map/while/body/eval_jaxpr/ppermute | solution.py:32
  176.5 58.9 %copy-start = (bf16[1,512,1024]{2,1,0:T(8,128)(2,1)S(1)}, bf16[1,512,1024]{2,1,0:T(8,128)(2,1)}, u32[]{:S(2)}) copy-start(bf16[1,512,1024]{2,1,0:T(8,128)(2,1)} %hid.1) | copy-start | bytes 3145732
  176.5 58.9 %copy-start.1 = (bf16[1,512,1024]{2,1,0:T(8,128)(2,1)S(1)}, bf16[1,512,1024]{2,1,0:T(8,128)(2,1)}, u32[]{:S(2)}) copy-start(bf16[1,512,1024]{2,1,0:T(8,128)(2,1)} %param.11) | copy-start | bytes 3145732
Sparse Core Ops, SparseCore 0:
  9.5 138.4 all-gather.1
  176.6 58.7 reduce-scatter.1

commit v2 on v1

v2 whole, which is shorter than its diff:
```python
import types

import jax
import jax.numpy as jnp
import numpy as np
from jax import lax
from jax.experimental import pallas as pl
from jax.experimental.pallas import tpu as pltpu
from jax.sharding import PartitionSpec as P

MODEL_WIDTH = 4096
HEAD_SIZE = 128
ROPE_BASE = 500000.0
NEG = -1e30
SCALE = float(np.log2(np.e) / np.sqrt(HEAD_SIZE))
MIB = 1024 * 1024

MESH = pl.DeviceIdType.MESH
SIDES = (1, -1)


def here():
    c, t, d = lax.axis_index("ctx"), lax.axis_index("tp"), lax.axis_index("dp")
    return c, t, d


class Net:
    def __init__(self, send_sems, recv_sems):
        self.send_sems, self.recv_sems = send_sems, recv_sems
        self.started = []

    def copy(self, k, src, dst, dev):
        c, t, d = dev
        return pltpu.make_async_remote_copy(
            src_ref=src,
            dst_ref=dst,
            send_sem=self.send_sems.at[k],
            recv_sem=self.recv_sems.at[k],
            device_id=(c, t, d),
            device_id_type=MESH,
        )

    def send(self, ref, dev, dst=None):
        k = len(self.started)
        copy = self.copy(k, ref, ref if dst is None else dst, dev)
        copy.start()
        self.started.append((copy, dev))
        return k

    def recv(self, k, ref):
        self.copy(k, ref, ref, self.started[k][1]).wait_recv()

    def finish(self):
        for copy, _ in self.started:
            copy.wait_send()


def places():
    c, t, d = here()
    z, xl = c // 2, c % 2
    c1 = c + 1 - 2 * xl
    t1 = t + 1 - 2 * (t % 2)
    t2 = (t + 2) % 4
    t3 = (t1 + 2) % 4
    return types.SimpleNamespace(
        c=c, t=t, d=d, z=z, xl=xl, xo=1 - xl, c1=c1, t1=t1, t2=t2, t3=t3,
        P=(c1, t, d), Q=(c1, t2, d), C=(c, t1, d), R=(c, t2, d), D=(c, t3, d),
        Y={s: (c, t, (d + s) % 4) for s in SIDES},
        Z={s: ((c + 2 * s) % 8, t, d) for s in SIDES},
        yo={s: (d - s) % 4 for s in SIDES},
        zo={s: (z - s) % 4 for s in SIDES},
        y2=(d + 2) % 4, z2=(z + 2) % 4,
        far=((c1, t1, d), (c1, t3, d), (c, t, (d + 2) % 4), ((c + 4) % 8, t, d)),
    )


def greet(m):
    barrier = pltpu.get_barrier_semaphore()
    others = [m.P, m.Q, m.C, m.R, m.D, m.Y[1], m.Y[-1], m.Z[1], m.Z[-1], *m.far]
    for dev in others:
        pl.semaphore_signal(barrier, inc=1, device_id=dev, device_id_type=MESH)
    pl.semaphore_wait(barrier, len(others))


def layer_kernel(
    hid, tgt, wq, wk, wv, wo, gain, order, row_cos, row_sin, block_cos, block_sin,
    out, loss_out,
    H, N, RH, W, acc, Q, KV, WO, AT, RA, num, peak, T, total, LB, ssem, rsem, lsem, osend, orecv,
):
    m = places()
    net = Net(ssem, rsem)
    c, t, d = m.c, m.t, m.d
    local = [
        pltpu.make_async_copy(wq, W.at[c, d, :, pl.ds(0, 512)], lsem.at[0]),
        pltpu.make_async_copy(wk, W.at[c, d, :, pl.ds(512, 128)], lsem.at[1]),
        pltpu.make_async_copy(wv, W.at[c, d, :, pl.ds(640, 128)], lsem.at[2]),
        pltpu.make_async_copy(hid.at[0], H.at[t], lsem.at[3]),
    ]
    for cp in local:
        cp.start()
    later = pltpu.make_async_copy(tgt.at[0], T, lsem.at[4])
    later.start()
    own_wo = pltpu.make_async_copy(wo, WO.at[m.xl * 4 + d, pl.ds(m.z * 512, 512)], lsem.at[5])
    greet(m)
    for cp in local:
        cp.wait()

    def pair(z):
        return pl.ds(2 * z, 2)

    qa = {1: pl.ds(0, 32), -1: pl.ds(32, 32)}
    qb = {1: pl.ds(64, 32), -1: pl.ds(96, 32)}
    ha, hb = pl.ds(0, 64), pl.ds(64, 64)
    parts = 2
    rows = 256 // parts

    kX = net.send(W.at[c, d], m.P)
    kY1 = {s: net.send(W.at[c, d], m.Y[s]) for s in SIDES}
    kZ1 = {s: net.send(W.at[c, d], m.Z[s]) for s in SIDES}
    kH0 = [net.send(H.at[t, pl.ds(i * rows, rows)], m.P, RH.at[0, pl.ds(i * rows, rows)]) for i in range(parts)]
    kH1 = [net.send(H.at[t, pl.ds(256 + i * rows, rows)], m.Q, RH.at[1, pl.ds(i * rows, rows)]) for i in range(parts)]
    kC = net.send(H.at[t], m.C)

    mine = WO.at[m.xl * 4 + d]
    block = WO.at[m.xl * 4 + d, pl.ds(t * 512, 512)]

    def meet(k):
        return pltpu.make_async_remote_copy(
            src_ref=wo, dst_ref=block, send_sem=osend.at[4], recv_sem=orecv.at[4 + k],
            device_id=(c, m.z, d), device_id_type=MESH,
        )

    @pl.when(t == m.z)
    def _():
        own_wo.start()

    @pl.when(t != m.z)
    def _():
        meet(t).start()

    net.recv(kX, W.at[m.c1, d])
    kY2 = {s: net.send(W.at[m.c1, d], m.Y[s]) for s in SIDES}
    kZ2 = {s: net.send(W.at[m.c1, d], m.Z[s]) for s in SIDES}

    fY, fZ, kY3, kZ3, kY4, kZ4 = {}, {}, {}, {}, {}, {}
    for s in SIDES:
        net.recv(kY1[s], W.at[c, m.yo[s]])
        net.recv(kZ1[s], W.at[2 * m.zo[s] + m.xl, d])
    for s in SIDES:
        net.recv(kY2[s], W.at[m.c1, m.yo[s]])
        kY3[s] = net.send(W.at[pair(m.z), m.yo[s], qa[s]], m.Y[s])
        net.recv(kZ2[s], W.at[2 * m.zo[s] + m.xo, d])
        kZ3[s] = net.send(W.at[pair(m.zo[s]), d, qb[s]], m.Z[s])
    for s in SIDES:
        for r in SIDES:
            kZ4[s, r] = net.send(W.at[pair(m.z), m.yo[s], ha], m.Z[r])
            kY4[s, r] = net.send(W.at[pair(m.zo[s]), d, hb], m.Y[r])

    def relay(i):
        net.recv(kH0[i], RH.at[0, pl.ds(i * rows, rows)])
        a = net.send(RH.at[0, pl.ds(i * rows, rows)], m.Q, H.at[t, pl.ds(i * rows, rows)])
        net.recv(kH1[i], RH.at[1, pl.ds(i * rows, rows)])
        b = net.send(RH.at[1, pl.ds(i * rows, rows)], m.P, H.at[m.t2, pl.ds(256 + i * rows, rows)])
        return a, b

    def landed(k):
        out = []
        for i in range(parts):
            for k_, lo in ((k[i][0], i * rows), (k[i][1], 256 + i * rows)):
                net.recv(k_, H.at[m.t2, pl.ds(lo, rows)])
                out.append((net.send(H.at[m.t2, pl.ds(lo, rows)], m.C), lo))
        return out

    kF = [relay(0)]
    kY6, kZ6 = {}, {}
    for s in SIDES:
        net.recv(kY3[s], W.at[pair(m.z), m.y2, qa[s]])
        net.recv(kZ3[s], W.at[pair(m.z2), d, qb[s]])
    for r in SIDES:
        kZ6[r] = net.send(W.at[pair(m.z), m.y2, ha], m.Z[r])
        kY6[r] = net.send(W.at[pair(m.z2), d, hb], m.Y[r])
    for s in SIDES:
        fZ[s, "own"] = net.send(W.at[pair(m.zo[s]), d, qa[s]], m.Z[s])
        fY[s, "own"] = net.send(W.at[pair(m.z), m.yo[s], qb[s]], m.Y[s])
    kF += [relay(i) for i in range(1, parts)]
    for s in SIDES:
        for r in SIDES:
            net.recv(kZ4[s, r], W.at[pair(m.zo[r]), m.yo[s], ha])
            fZ[r, s] = net.send(W.at[pair(m.zo[r]), m.yo[s], qa[r]], m.Z[r])
            net.recv(kY4[s, r], W.at[pair(m.zo[s]), m.yo[r], hb])
            fY[r, s] = net.send(W.at[pair(m.zo[s]), m.yo[r], qb[r]], m.Y[r])
    for r in SIDES:
        net.recv(kZ6[r], W.at[pair(m.zo[r]), m.y2, ha])
        fZ[r, "far"] = net.send(W.at[pair(m.zo[r]), m.y2, qa[r]], m.Z[r])
        net.recv(kY6[r], W.at[pair(m.z2), m.yo[r], hb])
        fY[r, "far"] = net.send(W.at[pair(m.z2), m.yo[r], qb[r]], m.Y[r])
    far = landed(kF)
    net.recv(kC, H.at[m.t1])
    for k, lo in far:
        net.recv(k, H.at[m.t3, pl.ds(lo, rows)])


    turn = (m.z - t + 4) % 4

    def along(k, ref, s):
        return pltpu.make_async_remote_copy(
            src_ref=ref, dst_ref=ref, send_sem=osend.at[k], recv_sem=orecv.at[k],
            device_id=m.Z[s], device_id_type=MESH,
        )

    low = WO.at[m.xl * 4 + d, pl.ds(0, 1024)]
    high = WO.at[m.xl * 4 + d, pl.ds(1024, 1024)]

    @pl.when(turn == 0)
    def _():
        own_wo.wait()
        for k in range(4):
            @pl.when(k != t)
            def _(k=k):
                there = WO.at[m.xl * 4 + d, pl.ds(k * 512, 512)]
                pltpu.make_async_remote_copy(
                    src_ref=there, dst_ref=there, send_sem=osend.at[4], recv_sem=orecv.at[4 + k],
                    device_id=(c, m.z, d), device_id_type=MESH,
                ).wait_recv()

        along(0, mine, 1).start()
        along(1, mine, -1).start()

    step = 64

    def norm(i, carry):
        at = pl.ds(pl.multiple_of(i * step, step), step)
        total = jnp.zeros((step, 1), jnp.float32)
        for b in range(4):
            x = H[b, at, :].astype(jnp.float32)
            total = total + jnp.sum(x * x, axis=1, keepdims=True)
        scale = lax.rsqrt(total * (1.0 / MODEL_WIDTH) + 1e-05)
        for b in range(4):
            x = H[b, at, :].astype(jnp.float32)
            g = gain[:, b * 1024 : (b + 1) * 1024]
            N[b, at, :] = (x * scale * g).astype(jnp.bfloat16)
        return carry

    lax.fori_loop(0, 512 // step, norm, 0)

    def chunk(z, first):
        for n in range(3):
            cols = pl.ds(n * 256, 256)
            w = W[pair(z), :, :, cols].reshape(1024, 256)
            part = jnp.dot(N[z], w, preferred_element_type=jnp.float32)
            if first:
                acc[:, cols] = part
            else:
                acc[:, cols] += part

    for r in SIDES:
        net.recv(fY[r, "own"], W.at[pair(m.z), m.y2, qb[r]])
    chunk(m.z, True)
    for s in SIDES:
        for r in SIDES:
            net.recv(fY[r, s], W.at[pair(m.zo[s]), m.y2, qb[r]])
    for s in SIDES:
        chunk(m.zo[s], False)
    for r in SIDES:
        net.recv(fZ[r, "own"], W.at[pair(m.z2), d, qa[r]])
        for s in SIDES:
            net.recv(fZ[r, s], W.at[pair(m.z2), m.yo[s], qa[r]])
        net.recv(fZ[r, "far"], W.at[pair(m.z2), m.y2, qa[r]])
        net.recv(fY[r, "far"], W.at[pair(m.z2), m.y2, qb[r]])
    chunk(m.z2, False)

    for s in range(2):
        where = order[2 * c + s]
        bc, bs = block_cos[pl.ds(where, 1), :], block_sin[pl.ds(where, 1), :]

        def rope(i, carry, s=s, bc=bc, bs=bs):
            rows_at = pl.ds(pl.multiple_of(i * step, step), step)
            at = pl.ds(pl.multiple_of(s * 256 + i * step, step), step)
            rc, rs = row_cos[rows_at, :], row_sin[rows_at, :]
            co = rc * bc - rs * bs
            si = rs * bc + rc * bs
            lane = lax.broadcasted_iota(jnp.int32, (step, 128), 1)
            si = jnp.where(lane < 64, -si, si)
            for h in range(5):
                x = acc[at, h * 128 : (h + 1) * 128]
                y = (x * co + pltpu.roll(x, 64, 1) * si).astype(jnp.bfloat16)
                if h < 4:
                    Q[h, at, :] = y
                else:
                    KV[c, 0, at, :] = y
            KV[c, 1, at, :] = acc[at, 640:768].astype(jnp.bfloat16)
            return carry

        lax.fori_loop(0, 256 // step, rope, 0)

    kv0 = net.send(KV.at[c], m.P)
    kv1 = {s: net.send(KV.at[c], m.Z[s]) for s in SIDES}

    @pl.when(turn == 1)
    def _():
        along(0, mine, 1).wait_recv()
        along(2, low, 1).start()

    @pl.when(turn == 3)
    def _():
        along(1, mine, -1).wait_recv()
        along(3, high, -1).start()

    def bias(s, ctx, half):
        return jnp.where(order[2 * ctx + half] < order[2 * c + s], 0.0, NEG).astype(jnp.float32)

    ones = jnp.ones((512, 128), jnp.bfloat16)
    row = lax.broadcasted_iota(jnp.int32, (256, 256), 0)
    col = lax.broadcasted_iota(jnp.int32, (256, 256), 1)

    def tile(h, s, ctx, first, lift):
        at = pl.ds(s * 256, 256)
        q = Q[h, at, :]
        scores = lax.dot_general(q, KV[ctx, 0], (((1,), (1,)), ((), ())), preferred_element_type=jnp.float32)
        halves = [scores[:, :256], scores[:, 256:]]
        if first:
            halves[s] = jnp.where(row >= col, halves[s], NEG)
        tops = [jnp.max(x, axis=1, keepdims=True) * SCALE + b for x, b in zip(halves, lift)]
        new = jnp.maximum(tops[0], tops[1])
        if not first:
            old = peak[h, at, :1]
            new = jnp.maximum(old, new)
        p = [jnp.exp2(x * SCALE + (b - new)).astype(jnp.bfloat16) for x, b in zip(halves, lift)]
        value = jnp.concatenate([KV[ctx, 1], ones], axis=1)
        part = jnp.dot(jnp.concatenate(p, axis=1), value, preferred_element_type=jnp.float32)
        if not first:
            part = num[h, at, :] * jnp.exp2(old - new) + part
        peak[h, at, :] = jnp.broadcast_to(new, (256, 128))
        num[h, at, :] = part

    def lifts(ctx, first):
        out = {}
        for s in range(2):
            out[s] = [bias(s, ctx, half) for half in range(2)]
            if first:
                out[s][s] = jnp.float32(0.0)
        return out

    def attend(ctx, first=False):
        lift = lifts(ctx, first)

        def head(h, carry):
            for s in range(2):
                tile(h, s, ctx, first, lift[s])
            return carry

        lax.fori_loop(0, 4, head, 0)

    attend(c, True)
    net.recv(kv0, KV.at[m.c1])
    kv2 = {s: net.send(KV.at[m.c1], m.Z[s]) for s in SIDES}

    @pl.when(turn == 2)
    def _():
        along(2, low, 1).wait_recv()
        along(3, high, -1).wait_recv()

    def strip(xl, y, s=None):
        return WO.at[xl * 4 + y] if s is None else WO.at[xl * 4 + y, pl.ds(0 if s == 1 else 1024, 1024)]

    wo0 = net.send(mine, m.P)
    wo1 = {s: net.send(mine, m.Y[s]) for s in SIDES}
    kv3, kv4, wo2, wo3, wo4 = {}, {}, {}, {}, {}
    part_of = {1: 0, -1: 1}
    for s in SIDES:
        there = 2 * m.zo[s] + m.xl
        net.recv(kv1[s], KV.at[there])
        kv3[s] = net.send(KV.at[there, part_of[s]], m.Z[s])
    for s in SIDES:
        attend(2 * m.zo[s] + m.xl)
    attend(m.c1)
    net.recv(wo0, strip(m.xo, d))
    for s in SIDES:
        wo2[s] = net.send(strip(m.xo, d), m.Y[s])
    for s in SIDES:
        there = 2 * m.zo[s] + m.xo
        net.recv(kv2[s], KV.at[there])
        kv4[s] = net.send(KV.at[there, part_of[s]], m.Z[s])
    for s in SIDES:
        attend(2 * m.zo[s] + m.xo)
    for s in SIDES:
        net.recv(wo1[s], strip(m.xl, m.yo[s]))
        wo3[s] = net.send(strip(m.xl, m.yo[s], s), m.Y[s])
    for s in SIDES:
        net.recv(kv3[s], KV.at[2 * m.z2 + m.xl, part_of[s]])
    for s in SIDES:
        net.recv(kv4[s], KV.at[2 * m.z2 + m.xo, part_of[s]])

    last = [(ctx, lifts(ctx, False)) for ctx in (2 * m.z2 + m.xl, 2 * m.z2 + m.xo)]
    top, bottom = pl.ds(0, 256), pl.ds(256, 256)
    kA = []
    for h in range(4):
        for ctx, lift in last:
            for s in range(2):
                tile(h, s, ctx, False, lift[s])
        both = num[h]
        AT[t, h] = (both[:, :128] / both[:, 128:]).astype(jnp.bfloat16)
        kA.append((
            net.send(AT.at[t, h, top], m.P, RA.at[0, h]),
            net.send(AT.at[t, h, bottom], m.Q, RA.at[1, h]),
            net.send(AT.at[t, h], m.C),
        ))
    for s in SIDES:
        net.recv(wo2[s], strip(m.xo, m.yo[s]))
        wo4[s] = net.send(strip(m.xo, m.yo[s], s), m.Y[s])
    kR = []
    for h in range(4):
        net.recv(kA[h][0], RA.at[0, h])
        a = net.send(RA.at[0, h], m.Q, AT.at[t, h, top])
        net.recv(kA[h][1], RA.at[1, h])
        kR.append((a, net.send(RA.at[1, h], m.P, AT.at[m.t2, h, bottom])))
    kD = []
    for h in range(4):
        net.recv(kR[h][0], AT.at[m.t2, h, top])
        net.recv(kR[h][1], AT.at[m.t2, h, bottom])
        kD.append(net.send(AT.at[m.t2, h], m.C))

    for s in SIDES:
        net.recv(wo3[s], strip(m.xl, m.y2, s))
        net.recv(wo4[s], strip(m.xo, m.y2, s))

    def project(b, first):
        left = jnp.concatenate([AT[b, h] for h in range(4)], axis=1)
        for j in range(4):
            right = jnp.concatenate([WO[2 * j + i, pl.ds(b * 512, 512), :] for i in range(2)], axis=1)
            part = jnp.dot(left, right, preferred_element_type=jnp.float32)
            cols = pl.ds(j * 256, 256)
            if first:
                total[:, cols] = part
            else:
                total[:, cols] += part

    project(t, True)
    for h in range(4):
        net.recv(kA[h][2], AT.at[m.t1, h])
    project(m.t1, False)
    project(m.t2, False)
    for h in range(4):
        net.recv(kD[h], AT.at[m.t3, h])
    project(m.t3, False)
    later.wait()

    def close(i, carry):
        at = pl.ds(pl.multiple_of(i * 32, 32), 32)
        branch = total[at, :].astype(jnp.bfloat16)
        out[0, at, :] = branch
        gap = H[t, at, :].astype(jnp.float32) + branch.astype(jnp.float32) - T[at, :].astype(jnp.float32)
        sq = gap * gap
        for r in range(4):
            for b in range(8):
                carry = carry + sq[r * 8 : (r + 1) * 8, b * 128 : (b + 1) * 128]
        return carry

    part = lax.fori_loop(0, 16, close, jnp.zeros((8, 128), jnp.float32))
    rings = (
        (8, m.xl * 4 + t, lambda i: (2 * m.z + i // 4, i % 4, d)),
        (4, d, lambda i: (c, t, i)),
        (4, m.z, lambda i: (2 * i + m.xl, t, d)),
    )
    for number, (size, me, device) in enumerate(rings):
        LB[number, me] = part
        ks = [net.send(LB.at[number, me], device((me + j) % size)) for j in range(1, size)]
        for j in range(1, size):
            net.recv(ks[j - 1], LB.at[number, (me + size - j) % size])
        part = LB[number, 0]
        for j in range(1, size):
            part = part + LB[number, j]
    loss_out[0, 0] = jnp.sum(part) / (4 * 4096 * MODEL_WIDTH)
    net.finish()

    @pl.when(t != m.z)
    def _():
        meet(t).wait_send()

    for k, ref, s, when in ((0, mine, 1, 0), (1, mine, -1, 0), (2, low, 1, 1), (3, high, -1, 3)):
        @pl.when(turn == when)
        def _(k=k, ref=ref, s=s):
            along(k, ref, s).wait_send()


def tables():
    freqs = ROPE_BASE ** (-(np.arange(64) * 2.0) / HEAD_SIZE)
    freqs = np.concatenate([freqs, freqs])[None, :]
    rows, blocks = np.arange(256)[:, None] * freqs, np.arange(16)[:, None] * 256 * freqs
    return [f(x).astype(np.float32) for x in (rows, blocks) for f in (np.cos, np.sin)]


def on_device(hidden, target, gain, w_query, w_key, value_matrix, w_out, block_order):
    any_spec = pl.BlockSpec(memory_space=pl.ANY)
    vmem = pl.BlockSpec(memory_space=pltpu.VMEM)
    smem = pl.BlockSpec(memory_space=pltpu.SMEM)
    bf16, f32 = jnp.bfloat16, jnp.float32
    branch, loss = pl.pallas_call(
        layer_kernel,
        out_shape=(jax.ShapeDtypeStruct((1, 512, 1024), bf16), jax.ShapeDtypeStruct((1, 1), f32)),
        in_specs=[any_spec] * 6 + [vmem, smem] + [vmem] * 4,
        out_specs=(vmem, smem),
        scratch_shapes=[
            pltpu.VMEM((4, 512, 1024), bf16),
            pltpu.VMEM((4, 512, 1024), bf16),
            pltpu.VMEM((2, 256, 1024), bf16),
            pltpu.VMEM((8, 4, 128, 768), bf16),
            pltpu.VMEM((512, 768), f32),
            pltpu.VMEM((4, 512, 128), bf16),
            pltpu.VMEM((8, 2, 512, 128), bf16),
            pltpu.VMEM((8, 2048, 128), bf16),
            pltpu.VMEM((4, 4, 512, 128), bf16),
            pltpu.VMEM((2, 4, 256, 128), bf16),
            pltpu.VMEM((4, 512, 256), f32),
            pltpu.VMEM((4, 512, 128), f32),
            pltpu.VMEM((512, 1024), bf16),
            pltpu.VMEM((512, 1024), f32),
            pltpu.VMEM((3, 8, 8, 128), f32),
            pltpu.SemaphoreType.DMA((128,)),
            pltpu.SemaphoreType.DMA((128,)),
            pltpu.SemaphoreType.DMA((8,)),
            pltpu.SemaphoreType.DMA((8,)),
            pltpu.SemaphoreType.DMA((8,)),
        ],
        compiler_params=pltpu.CompilerParams(
            collective_id=0, has_side_effects=True, vmem_limit_bytes=60 * MIB
        ),
        name="layer",
    )(hidden, target, w_query, w_key, value_matrix, w_out, gain[None, :], block_order, *(jnp.asarray(x) for x in tables()))
    return branch, loss.reshape(())


def solution(mesh):
    placed = (
        P("dp", "ctx", "tp"), P("dp", "ctx", "tp"), P(), P(("ctx", "dp"), "tp"), P(("ctx", "dp"), "tp"),
        P(("ctx", "dp"), "tp"), P("tp", ("ctx", "dp")), P(),
    )
    return jax.shard_map(
        on_device, mesh=mesh, in_specs=placed, out_specs=(P("dp", "ctx", "tp"), P()), check_vma=False
    )
```

time: 312 us -> 128 us (0.41)
  waiting for transfers between devices: 124 us -> 0 us
  blocking collectives: 65.1 us -> 0 us
  Pallas kernels: 59.6 us -> 123 us
  matrix products: 28.2 us -> 0 us
  other arithmetic: 16.3 us -> 0 us
  between operations: 15.9 us -> 2.33 us
    psum x1 -> x0, blocking collectives: 65.1 us -> none  [on_device(): squares = lax.psum(jnp.sum(resid * resid), CTX_TP_DP)]
    ppermute x7 -> x0, waiting for transfers between devices: 64.5 us -> none  [shifted(): lax.ppermute(value, axis, [(i, (i + by) % peers) for i in range(peers)])]
    pallas_call x1, Pallas kernels: 59.6 us -> 123 us  [on_device(): pl.pallas_call(layer_kernel, out_shape=(jax.ShapeDtypeStruct((1, 512, 102...]
    reduce_scatter x1 -> x0, waiting for transfers between devices: 58.9 us -> none  [on_device(): lax.psum_scatter(terms.astype(jnp.bfloat16), TP, scatter_dimension=1, til...]
    dot_general x17 -> x0, matrix products: 28.2 us -> none  [the longest x8 14.7 us: attend(): jnp.einsum('cgqk,kcd->qcgd', weights.astype(jnp.bfloat16), pair[1], prefe...]
    reduce_sum x17 -> x0, other arithmetic: 12.1 us -> none  [the longest x8 8.34 us: attend(): total = total * factor + jnp.sum(weights, axis=-1)]
  transfers between devices with their start and end apart: 9 -> 0, of which waited for: 8 -> 0; matrix products, arithmetic and copies ran while one was open for 12% -> 0% of each run, Pallas kernels for 19% -> 0%
where the time goes in v2:
time: 128 us
  Pallas kernels  123 us (96%)
  between operations  2.33 us (2%)
  local copies, waits for them, and re-layouts  2.26 us (2%)
    pallas_call x1, Pallas kernels, on_device(): pl.pallas_call(layer_kernel, out_shape=(jax.ShapeDtypeStruct((1, 512, 102...  123 us

profile of v2, /device:TPU:1, one launch (start us, length us, event | category | flops | bytes accessed | tf_op | source)
XLA Modules:
  0.0 127.5 jit_solution(943738933236724176)
XLA Ops:
  0.6 122.9 %layer.1 = (bf16[1,512,1024]{2,1,0:T(8,128)(2,1)}, f32[1,1]{1,0:T(1,128)}) custom-call(bf16[1,512,1024]{2,1,0:T(8,128)(2,1)} %hid.1, bf16[1,512,1024]{2,1,0:T(8,128)(2,1)} %tgt.1, bf16[128,512]{1,0:T(8,128)(2,1)} %wq.1, bf16[128,128]{1,0:T(8,128)(2,1)} %wk.1, bf16[128,128]{1,0:T(8,128)(2,1)} %wv.1, bf16[512,128]{1,0:T(8,128)(2,1)} %wo.1, f32[1,4096]{1,0:T(1,128)} %bitcast.2, ...), custom_call_target="tpu_custom_call" | custom-call | tf_op jit(solution)/shard_map/layer/pallas_call | solution.py:498
  123.6 2.3 %copy.16 = bf16[1,512,1024]{2,1,0:T(8,128)(2,1)} copy(bf16[1,512,1024]{2,1,0:T(8,128)(2,1)} %get-tuple-element.8) | data formatting | bytes 2097152

commit v3 on v2

v3 whole, which is shorter than its diff:
```python
import types

import jax
import jax.numpy as jnp
import numpy as np
from jax import lax
from jax.experimental import pallas as pl
from jax.experimental.pallas import tpu as pltpu
from jax.sharding import PartitionSpec as P

MODEL_WIDTH = 4096
HEAD_SIZE = 128
ROPE_BASE = 500000.0
NEG = -1e30
SCALE = float(np.log2(np.e) / np.sqrt(HEAD_SIZE))
MIB = 1024 * 1024
POOL = 40
COPIES = 120

MESH = pl.DeviceIdType.MESH
SIDES = (1, -1)


def here():
    c, t, d = lax.axis_index("ctx"), lax.axis_index("tp"), lax.axis_index("dp")
    return c, t, d


class Net:
    def __init__(self, send_sems, recv_sems):
        self.send_sems, self.recv_sems = send_sems, recv_sems
        self.started = []

    def copy(self, k, src, dst, dev):
        c, t, d = dev
        return pltpu.make_async_remote_copy(
            src_ref=src,
            dst_ref=dst,
            send_sem=self.send_sems.at[k % POOL],
            recv_sem=self.recv_sems.at[k],
            device_id=(c, t, d),
            device_id_type=MESH,
        )

    def plan(self, ref, dev, dst=None):
        k = len(self.started)
        if k >= POOL:
            self.started[k - POOL][0].wait_send()
        self.started.append((self.copy(k, ref, ref if dst is None else dst, dev), dev))
        return k

    def start(self, k):
        self.started[k][0].start()

    def send(self, ref, dev, dst=None):
        k = self.plan(ref, dev, dst)
        self.start(k)
        return k

    def recv(self, k, ref):
        self.copy(k, ref, ref, self.started[k][1]).wait_recv()

    def finish(self):
        assert len(self.started) <= COPIES
        for copy, _ in self.started[-POOL:]:
            copy.wait_send()


def places():
    c, t, d = here()
    z, xl = c // 2, c % 2
    c1 = c + 1 - 2 * xl
    t1 = t + 1 - 2 * (t % 2)
    t2 = (t + 2) % 4
    t3 = (t1 + 2) % 4
    return types.SimpleNamespace(
        c=c, t=t, d=d, z=z, xl=xl, xo=1 - xl, c1=c1, t1=t1, t2=t2, t3=t3,
        P=(c1, t, d), Q=(c1, t2, d), C=(c, t1, d), R=(c, t2, d), D=(c, t3, d),
        Y={s: (c, t, (d + s) % 4) for s in SIDES},
        Z={s: ((c + 2 * s) % 8, t, d) for s in SIDES},
        yo={s: (d - s) % 4 for s in SIDES},
        zo={s: (z - s) % 4 for s in SIDES},
        y2=(d + 2) % 4, z2=(z + 2) % 4,
    )


def greet(m):
    barrier = pltpu.get_barrier_semaphore()
    others = [m.P, m.Q, m.C, m.R, m.D, m.Y[1], m.Y[-1], m.Z[1], m.Z[-1]]
    for dev in others:
        pl.semaphore_signal(barrier, inc=1, device_id=dev, device_id_type=MESH)
    pl.semaphore_wait(barrier, len(others))


def layer_kernel(
    hid, tgt, wq, wk, wv, wo, gain, order, turn_cos, turn_sin, block_cos, block_sin,
    out, loss_out,
    H, N, RH, W, acc, Q, KV, WO, AT, RA, num, peak, T, total, LB, row_cos, row_sin, ssem, rsem, lsem, osend, orecv,
):
    m = places()
    net = Net(ssem, rsem)
    c, t, d = m.c, m.t, m.d
    local = [
        pltpu.make_async_copy(wq, W.at[c, d, :, pl.ds(0, 512)], lsem.at[0]),
        pltpu.make_async_copy(wk, W.at[c, d, :, pl.ds(512, 128)], lsem.at[1]),
        pltpu.make_async_copy(wv, W.at[c, d, :, pl.ds(640, 128)], lsem.at[2]),
        pltpu.make_async_copy(hid.at[0], H.at[t], lsem.at[3]),
    ]
    for cp in local:
        cp.start()
    later = pltpu.make_async_copy(tgt.at[0], T, lsem.at[4])
    later.start()
    turns = [
        pltpu.make_async_copy(turn_cos, row_cos, lsem.at[6]),
        pltpu.make_async_copy(turn_sin, row_sin, lsem.at[7]),
    ]
    for cp in turns:
        cp.start()
    own_wo = pltpu.make_async_copy(wo, WO.at[m.xl * 4 + d, pl.ds(m.z * 512, 512)], lsem.at[5])
    greet(m)
    for cp in local:
        cp.wait()

    def pair(z):
        return pl.ds(2 * z, 2)

    qa = {1: pl.ds(0, 32), -1: pl.ds(32, 32)}
    qb = {1: pl.ds(64, 32), -1: pl.ds(96, 32)}
    ha, hb = pl.ds(0, 64), pl.ds(64, 64)
    parts = 4
    rows = 256 // parts

    kX = net.send(W.at[c, d], m.P)
    kY1 = {s: net.send(W.at[c, d], m.Y[s]) for s in SIDES}
    kZ1 = {s: net.send(W.at[c, d], m.Z[s]) for s in SIDES}
    kH0 = [net.send(H.at[t, pl.ds(i * rows, rows)], m.P, RH.at[0, pl.ds(i * rows, rows)]) for i in range(parts)]
    kH1 = [net.send(H.at[t, pl.ds(256 + i * rows, rows)], m.Q, RH.at[1, pl.ds(i * rows, rows)]) for i in range(parts)]
    kC = net.send(H.at[t], m.C)

    mine = WO.at[m.xl * 4 + d]
    block = WO.at[m.xl * 4 + d, pl.ds(t * 512, 512)]

    def meet(k):
        return pltpu.make_async_remote_copy(
            src_ref=wo, dst_ref=block, send_sem=osend.at[4], recv_sem=orecv.at[4 + k],
            device_id=(c, m.z, d), device_id_type=MESH,
        )

    @pl.when(t == m.z)
    def _():
        own_wo.start()

    @pl.when(t != m.z)
    def _():
        meet(t).start()

    net.recv(kX, W.at[m.c1, d])
    kY2 = {s: net.send(W.at[m.c1, d], m.Y[s]) for s in SIDES}
    kZ2 = {s: net.send(W.at[m.c1, d], m.Z[s]) for s in SIDES}

    def relay(i):
        net.recv(kH0[i], RH.at[0, pl.ds(i * rows, rows)])
        a = net.send(RH.at[0, pl.ds(i * rows, rows)], m.Q, H.at[t, pl.ds(i * rows, rows)])
        net.recv(kH1[i], RH.at[1, pl.ds(i * rows, rows)])
        b = net.send(RH.at[1, pl.ds(i * rows, rows)], m.P, H.at[m.t2, pl.ds(256 + i * rows, rows)])
        return a, b

    far = []

    def landed(i):
        for k_, lo in ((kF[i][0], i * rows), (kF[i][1], 256 + i * rows)):
            net.recv(k_, H.at[m.t2, pl.ds(lo, rows)])
            far.append((net.send(H.at[m.t2, pl.ds(lo, rows)], m.C), lo))

    kF = []
    fY, fZ, kY3, kZ3, kY4, kZ4 = {}, {}, {}, {}, {}, {}
    for s in SIDES:
        net.recv(kY1[s], W.at[c, m.yo[s]])
        net.recv(kZ1[s], W.at[2 * m.zo[s] + m.xl, d])
    kF.append(relay(0))
    for s in SIDES:
        net.recv(kY2[s], W.at[m.c1, m.yo[s]])
        kY3[s] = net.send(W.at[pair(m.z), m.yo[s], qa[s]], m.Y[s])
        net.recv(kZ2[s], W.at[2 * m.zo[s] + m.xo, d])
        kZ3[s] = net.send(W.at[pair(m.zo[s]), d, qb[s]], m.Z[s])
    for s in SIDES:
        for r in SIDES:
            kZ4[s, r] = net.send(W.at[pair(m.z), m.yo[s], ha], m.Z[r])
            kY4[s, r] = net.send(W.at[pair(m.zo[s]), d, hb], m.Y[r])

    kF += [relay(1), relay(2)]
    kY6, kZ6 = {}, {}
    for s in SIDES:
        net.recv(kY3[s], W.at[pair(m.z), m.y2, qa[s]])
        net.recv(kZ3[s], W.at[pair(m.z2), d, qb[s]])
    for r in SIDES:
        kZ6[r] = net.send(W.at[pair(m.z), m.y2, ha], m.Z[r])
        kY6[r] = net.send(W.at[pair(m.z2), d, hb], m.Y[r])
    for s in SIDES:
        fZ[s, "own"] = net.send(W.at[pair(m.zo[s]), d, qa[s]], m.Z[s])
        fY[s, "own"] = net.send(W.at[pair(m.z), m.yo[s], qb[s]], m.Y[s])
    kF.append(relay(3))
    for s in SIDES:
        for r in SIDES:
            net.recv(kZ4[s, r], W.at[pair(m.zo[r]), m.yo[s], ha])
            fZ[r, s] = net.send(W.at[pair(m.zo[r]), m.yo[s], qa[r]], m.Z[r])
            net.recv(kY4[s, r], W.at[pair(m.zo[s]), m.yo[r], hb])
            fY[r, s] = net.send(W.at[pair(m.zo[s]), m.yo[r], qb[r]], m.Y[r])
    landed(0)
    landed(1)
    landed(2)
    landed(3)
    for r in SIDES:
        net.recv(kZ6[r], W.at[pair(m.zo[r]), m.y2, ha])
        fZ[r, "far"] = net.send(W.at[pair(m.zo[r]), m.y2, qa[r]], m.Z[r])
        net.recv(kY6[r], W.at[pair(m.z2), m.yo[r], hb])
        fY[r, "far"] = net.send(W.at[pair(m.z2), m.yo[r], qb[r]], m.Y[r])
    turn = (m.z - t + 4) % 4

    def along(k, ref, s):
        return pltpu.make_async_remote_copy(
            src_ref=ref, dst_ref=ref, send_sem=osend.at[k], recv_sem=orecv.at[k],
            device_id=m.Z[s], device_id_type=MESH,
        )

    low = WO.at[m.xl * 4 + d, pl.ds(0, 1024)]
    high = WO.at[m.xl * 4 + d, pl.ds(1024, 1024)]

    @pl.when(turn == 0)
    def _():
        own_wo.wait()
        for k in range(4):
            @pl.when(k != t)
            def _(k=k):
                there = WO.at[m.xl * 4 + d, pl.ds(k * 512, 512)]
                pltpu.make_async_remote_copy(
                    src_ref=there, dst_ref=there, send_sem=osend.at[4], recv_sem=orecv.at[4 + k],
                    device_id=(c, m.z, d), device_id_type=MESH,
                ).wait_recv()

        along(0, mine, 1).start()
        along(1, mine, -1).start()

    def strip(xl, y, s=None):
        return WO.at[xl * 4 + y] if s is None else WO.at[xl * 4 + y, pl.ds(0 if s == 1 else 1024, 1024)]

    wo1 = {s: net.plan(mine, m.Y[s]) for s in SIDES}

    @pl.when(turn == 0)
    def _():
        for s in SIDES:
            net.start(wo1[s])

    net.recv(kC, H.at[m.t1])
    for k, lo in far:
        net.recv(k, H.at[m.t3, pl.ds(lo, rows)])


    step = 64

    def norm(i, carry):
        at = pl.ds(pl.multiple_of(i * step, step), step)
        total = jnp.zeros((step, 1), jnp.float32)
        for b in range(4):
            x = H[b, at, :].astype(jnp.float32)
            total = total + jnp.sum(x * x, axis=1, keepdims=True)
        scale = lax.rsqrt(total * (1.0 / MODEL_WIDTH) + 1e-05)
        for b in range(4):
            x = H[b, at, :].astype(jnp.float32)
            g = gain[:, b * 1024 : (b + 1) * 1024]
            N[b, at, :] = (x * scale * g).astype(jnp.bfloat16)
        return carry

    lax.fori_loop(0, 512 // step, norm, 0)

    def columns(zs, lo):
        cols = pl.ds(lo, 256)
        sums = None
        for z in zs:
            w = W[pair(z), :, :, cols].reshape(1024, 256)
            part = jnp.dot(N[z], w, preferred_element_type=jnp.float32)
            sums = part if sums is None else sums + part
        return sums

    for r in SIDES:
        net.recv(fY[r, "own"], W.at[pair(m.z), m.y2, qb[r]])
        for s in SIDES:
            net.recv(fY[r, s], W.at[pair(m.zo[s]), m.y2, qb[r]])
    acc[:, pl.ds(512, 256)] = columns((m.z, m.zo[1], m.zo[-1]), 512)

    for r in SIDES:
        net.recv(fZ[r, "own"], W.at[pair(m.z2), d, qa[r]])
        for s in SIDES:
            net.recv(fZ[r, s], W.at[pair(m.z2), m.yo[s], qa[r]])
        net.recv(fZ[r, "far"], W.at[pair(m.z2), m.y2, qa[r]])
        net.recv(fY[r, "far"], W.at[pair(m.z2), m.y2, qb[r]])
    acc[:, pl.ds(512, 256)] += columns((m.z2,), 512)
    for cp in turns:
        cp.wait()

    def rotate(heads):
        for s in range(2):
            where = order[2 * c + s]
            bc, bs = block_cos[pl.ds(where, 1), :], block_sin[pl.ds(where, 1), :]

            def rope(i, carry, s=s, bc=bc, bs=bs):
                rows_at = pl.ds(pl.multiple_of(i * step, step), step)
                at = pl.ds(pl.multiple_of(s * 256 + i * step, step), step)
                rc, rs = row_cos[rows_at, :], row_sin[rows_at, :]
                co = rc * bc - rs * bs
                si = rs * bc + rc * bs
                lane = lax.broadcasted_iota(jnp.int32, (step, 128), 1)
                si = jnp.where(lane < 64, -si, si)
                for h in heads:
                    x = acc[at, h * 128 : (h + 1) * 128]
                    y = (x * co + pltpu.roll(x, 64, 1) * si).astype(jnp.bfloat16)
                    if h < 4:
                        Q[h, at, :] = y
                    else:
                        KV[c, 0, at, :] = y
                        KV[c, 1, at, :] = acc[at, 640:768].astype(jnp.bfloat16)
                return carry

            lax.fori_loop(0, 256 // step, rope, 0)

    rotate((4,))
    kv0 = net.send(KV.at[c], m.P)
    kv1 = {s: net.send(KV.at[c], m.Z[s]) for s in SIDES}

    wo0 = {s: net.plan(strip(m.xl, d, s), m.P) for s in SIDES}

    @pl.when(turn == 0)
    def _():
        for s in SIDES:
            net.start(wo0[s])

    acc[:, pl.ds(0, 256)] = columns((m.z, m.zo[1], m.zo[-1], m.z2), 0)

    @pl.when(turn == 1)
    def _():
        along(0, mine, 1).wait_recv()
        along(2, low, 1).start()

    @pl.when(turn == 3)
    def _():
        along(1, mine, -1).wait_recv()
        along(3, high, -1).start()

    @pl.when(turn % 2 == 1)
    def _():
        for s in SIDES:
            net.start(wo1[s])
        for s in SIDES:
            net.start(wo0[s])

    acc[:, pl.ds(256, 256)] = columns((m.z, m.zo[1], m.zo[-1], m.z2), 256)
    rotate((0, 1, 2, 3))

    def bias(s, ctx, half):
        return jnp.where(order[2 * ctx + half] < order[2 * c + s], 0.0, NEG).astype(jnp.float32)

    ones = jnp.ones((512, 128), jnp.bfloat16)
    row = lax.broadcasted_iota(jnp.int32, (256, 256), 0)
    col = lax.broadcasted_iota(jnp.int32, (256, 256), 1)

    def tile(h, s, at, size, ctxs, first, lift):
        q = Q[h, at, :]
        pieces = []
        for ctx, lift_ in zip(ctxs, lift):
            x = lax.dot_general(q, KV[ctx, 0], (((1,), (1,)), ((), ())), preferred_element_type=jnp.float32)
            for half in range(2):
                y = x[:, half * 256 : (half + 1) * 256]
                if first and half == s:
                    y = jnp.where(row >= col, y, NEG)
                pieces.append((y, lift_[s][half]))
        top = None
        for y, b in pieces:
            e = jnp.maximum(y[:, :128], y[:, 128:]) + b
            top = e if top is None else jnp.maximum(top, e)
        new = jnp.broadcast_to(jnp.max(top, axis=1, keepdims=True), (size, 128))
        if not first:
            old = peak[h, at, :]
            new = jnp.maximum(old, new)
        level = new * SCALE
        p = []
        for y, b in pieces:
            down = b - level
            p.append(jnp.exp2(y * SCALE + jnp.concatenate([down, down], axis=1)).astype(jnp.bfloat16))
        part = None
        for i, ctx in enumerate(ctxs):
            value = jnp.concatenate([KV[ctx, 1], ones], axis=1)
            one = jnp.dot(jnp.concatenate(p[2 * i : 2 * i + 2], axis=1), value, preferred_element_type=jnp.float32)
            part = one if part is None else part + one
        if not first:
            factor = jnp.exp2((old - new) * SCALE)
            part = num[h, at, :] * jnp.concatenate([factor, factor], axis=1) + part
        return new, part

    def lifts(ctxs, first=False):
        out = []
        for ctx in ctxs:
            out.append([[jnp.float32(0.0) if first and s == half else bias(s, ctx, half) for half in range(2)] for s in range(2)])
        return out

    def tiles(h, ctxs, first, lift):
        size = 128 if len(ctxs) > 1 else 256
        out = []
        for s in range(2):
            for at in range(s * 256, (s + 1) * 256, size):
                at = pl.ds(at, size)
                out.append((at, tile(h, s, at, size, ctxs, first, lift)))
        return out

    def attend(ctxs, first=False):
        lift = lifts(ctxs, first)
        for h in range(4):
            for at, (new, part) in tiles(h, ctxs, first, lift):
                peak[h, at, :], num[h, at, :] = new, part

    kv2, kv3, kv4, kv5, wo2, wo3, wo4 = {}, {}, {}, {}, {}, {}, {}
    part_of = {1: 0, -1: 1}
    both, early, late = pl.ds(0, 2), pl.ds(0, 320), pl.ds(320, 192)
    attend((c,), True)

    @pl.when(turn == 2)
    def _():
        along(2, low, 1).wait_recv()
        along(3, high, -1).wait_recv()
        for s in SIDES:
            net.start(wo1[s])
        for s in SIDES:
            net.start(wo0[s])


    net.recv(kv0, KV.at[m.c1])
    for s in SIDES:
        kv2[s] = net.send(KV.at[m.c1, both, early], m.Z[s])
    for s in SIDES:
        there = 2 * m.zo[s] + m.xl
        net.recv(kv1[s], KV.at[there])
        kv3[s] = net.send(KV.at[there, part_of[s]], m.Z[s])
        kv5[s] = net.send(KV.at[there, both, late], m.P)
    attend([2 * m.zo[s] + m.xl for s in SIDES])
    for s in SIDES:
        wo3[s] = net.plan(strip(m.xl, m.yo[s], s), m.Y[s])

    def pass_on():
        for s in SIDES:
            net.recv(wo1[s], strip(m.xl, m.yo[s]))
            net.start(wo3[s])

    attend((m.c1,))
    pass_on()
    for s in SIDES:
        there = 2 * m.zo[s] + m.xo
        net.recv(kv2[s], KV.at[there, both, early])
        kv4[s] = net.send(KV.at[there, part_of[s], early], m.Z[s])
    for s in SIDES:
        net.recv(kv3[s], KV.at[2 * m.z2 + m.xl, part_of[s]])
    kv6 = net.send(KV.at[2 * m.z2 + m.xl, both, late], m.P)
    attend((2 * m.z2 + m.xl,))
    for r in SIDES:
        for s in SIDES:
            wo2[r, s] = net.plan(strip(m.xo, d, r), m.Y[s])

    def cross():
        for r in SIDES:
            net.recv(wo0[r], strip(m.xo, d, r))
            for s in SIDES:
                net.start(wo2[r, s])

    cross()
    for s in SIDES:
        net.recv(kv5[s], KV.at[2 * m.zo[s] + m.xo, both, late])
    attend([2 * m.zo[s] + m.xo for s in SIDES])

    for s in SIDES:
        net.recv(kv4[s], KV.at[2 * m.z2 + m.xo, part_of[s], early])
    net.recv(kv6, KV.at[2 * m.z2 + m.xo, both, late])

    last = (2 * m.z2 + m.xo,)
    lift = lifts(last)
    top, bottom = pl.ds(0, 256), pl.ds(256, 256)
    kA = []
    for h in range(4):
        for at, (_, part) in tiles(h, last, False, lift):
            AT[t, h, at, :] = (part[:, :128] / part[:, 128:]).astype(jnp.bfloat16)
        ks = [net.send(AT.at[t, h, pl.ds(s * 256, 256)], (m.P, m.Q)[s], RA.at[s, h]) for s in range(2)]
        ks.append(net.send(AT.at[t, h], m.C))
        kA.append(ks)
    kR = []
    for h in range(4):
        net.recv(kA[h][0], RA.at[0, h])
        a = net.send(RA.at[0, h], m.Q, AT.at[t, h, top])
        net.recv(kA[h][1], RA.at[1, h])
        kR.append((a, net.send(RA.at[1, h], m.P, AT.at[m.t2, h, bottom])))
        if h == 3:
            for s in SIDES:
                net.recv(wo2[s, s], strip(m.xo, m.yo[s], s))
                wo4[s] = net.send(strip(m.xo, m.yo[s], s), m.Y[s])
    kD = []
    for h in range(4):
        net.recv(kR[h][0], AT.at[m.t2, h, top])
        net.recv(kR[h][1], AT.at[m.t2, h, bottom])
        kD.append(net.send(AT.at[m.t2, h], m.C))

    soon = [[(m.xl, d), (m.xl, m.yo[1])], [(m.xl, m.yo[-1]), (m.xl, m.y2)], [(m.xo, d), (m.xo, m.yo[1])]]
    last_two = [(m.xo, m.yo[-1]), (m.xo, m.y2)]

    def product(bs, two):
        left = jnp.concatenate([AT[b, h] for b in bs for h in range(4)], axis=1)
        right = jnp.concatenate(
            [jnp.concatenate([WO[xl * 4 + y, pl.ds(b * 512, 512), :] for b in bs], axis=0) for xl, y in two], axis=1
        )
        return jnp.dot(left, right, preferred_element_type=jnp.float32)

    def project(bs, first=False):
        for two in soon:
            part = product(bs, two)
            for i, (xl, y) in enumerate(two):
                cols = pl.ds(pl.multiple_of((xl * 4 + y) * 128, 128), 128)
                piece = part[:, i * 128 : (i + 1) * 128]
                if first:
                    total[:, cols] = piece
                else:
                    total[:, cols] += piece

    for s in SIDES:
        net.recv(wo3[s], strip(m.xl, m.y2, s))
    net.recv(wo2[-1, 1], strip(m.xo, m.yo[1], -1))
    net.recv(wo2[1, -1], strip(m.xo, m.yo[-1], 1))
    for h in range(4):
        net.recv(kA[h][2], AT.at[m.t1, h])
    project((t, m.t1), True)
    project((m.t2,))
    for h in range(4):
        net.recv(kD[h], AT.at[m.t3, h])
    project((m.t3,))
    for s in SIDES:
        net.recv(wo4[s], strip(m.xo, m.y2, s))
    part = product((t, m.t1, m.t2, m.t3), last_two)
    for i, (xl, y) in enumerate(last_two):
        total[:, pl.ds(pl.multiple_of((xl * 4 + y) * 128, 128), 128)] = part[:, i * 128 : (i + 1) * 128]
    later.wait()

    def close(i, carry):
        at = pl.ds(pl.multiple_of(i * 32, 32), 32)
        branch = total[at, :].astype(jnp.bfloat16)
        out[at, :] = branch
        gap = H[t, at, :].astype(jnp.float32) + branch.astype(jnp.float32) - T[at, :].astype(jnp.float32)
        sq = gap * gap
        for r in range(4):
            for b in range(8):
                carry = carry + sq[r * 8 : (r + 1) * 8, b * 128 : (b + 1) * 128]
        return carry

    part = lax.fori_loop(0, 16, close, jnp.zeros((8, 128), jnp.float32))
    rings = (
        (8, m.xl * 4 + t, lambda i: (2 * m.z + i // 4, i % 4, d)),
        (16, m.z * 4 + d, lambda i: (2 * (i // 4) + m.xl, t, i % 4)),
    )
    for number, (size, me, device) in enumerate(rings):
        LB[number, me] = part
        for j in range(1, size):
            pltpu.make_async_remote_copy(
                src_ref=LB.at[number, me], dst_ref=LB.at[number, me], send_sem=osend.at[5 + number],
                recv_sem=orecv.at[8 + number], device_id=device((me + j) % size), device_id_type=MESH,
            ).start()
        others = LB.at[number, pl.ds(0, size - 1)]
        pltpu.make_async_copy(others, others, orecv.at[8 + number]).wait()
        pltpu.make_async_copy(others, others, osend.at[5 + number]).wait()
        part = LB[number, 0]
        for j in range(1, size):
            part = part + LB[number, j]
    loss_out[0, 0] = jnp.sum(part) / (4 * 4096 * MODEL_WIDTH)
    net.finish()

    @pl.when(t != m.z)
    def _():
        meet(t).wait_send()

    for k, ref, s, when in ((0, mine, 1, 0), (1, mine, -1, 0), (2, low, 1, 1), (3, high, -1, 3)):
        @pl.when(turn == when)
        def _(k=k, ref=ref, s=s):
            along(k, ref, s).wait_send()


def tables():
    freqs = ROPE_BASE ** (-(np.arange(64) * 2.0) / HEAD_SIZE)
    freqs = np.concatenate([freqs, freqs])[None, :]
    rows, blocks = np.arange(256)[:, None] * freqs, np.arange(16)[:, None] * 256 * freqs
    return [f(x).astype(np.float32) for x in (rows, blocks) for f in (np.cos, np.sin)]


def on_device(hidden, target, gain, w_query, w_key, value_matrix, w_out, block_order):
    any_spec = pl.BlockSpec(memory_space=pl.ANY)
    vmem = pl.BlockSpec(memory_space=pltpu.VMEM)
    smem = pl.BlockSpec(memory_space=pltpu.SMEM)
    bf16, f32 = jnp.bfloat16, jnp.float32
    branch, loss = pl.pallas_call(
        layer_kernel,
        out_shape=(pltpu.VMEM((512, 1024), bf16), jax.ShapeDtypeStruct((1, 1), f32)),
        in_specs=[any_spec] * 6 + [vmem, smem, any_spec, any_spec, vmem, vmem],
        out_specs=(vmem, smem),
        scratch_shapes=[
            pltpu.VMEM((4, 512, 1024), bf16),
            pltpu.VMEM((4, 512, 1024), bf16),
            pltpu.VMEM((2, 256, 1024), bf16),
            pltpu.VMEM((8, 4, 128, 768), bf16),
            pltpu.VMEM((512, 768), f32),
            pltpu.VMEM((4, 512, 128), bf16),
            pltpu.VMEM((8, 2, 512, 128), bf16),
            pltpu.VMEM((8, 2048, 128), bf16),
            pltpu.VMEM((4, 4, 512, 128), bf16),
            pltpu.VMEM((2, 4, 256, 128), bf16),
            pltpu.VMEM((4, 512, 256), f32),
            pltpu.VMEM((4, 512, 128), f32),
            pltpu.VMEM((512, 1024), bf16),
            pltpu.VMEM((512, 1024), f32),
            pltpu.VMEM((2, 16, 8, 128), f32),
            pltpu.VMEM((256, 128), f32),
            pltpu.VMEM((256, 128), f32),
            pltpu.SemaphoreType.DMA((POOL,)),
            pltpu.SemaphoreType.DMA((COPIES,)),
            pltpu.SemaphoreType.DMA((8,)),
            pltpu.SemaphoreType.DMA((8,)),
            pltpu.SemaphoreType.DMA((10,)),
        ],
        compiler_params=pltpu.CompilerParams(
            collective_id=0, has_side_effects=True, vmem_limit_bytes=60 * MIB
        ),
        name="layer",
    )(hidden, target, w_query, w_key, value_matrix, w_out, gain[None, :], block_order, *(jnp.asarray(x) for x in tables()))
    return branch[None], loss.reshape(())


def solution(mesh):
    placed = (
        P("dp", "ctx", "tp"), P("dp", "ctx", "tp"), P(), P(("ctx", "dp"), "tp"), P(("ctx", "dp"), "tp"),
        P(("ctx", "dp"), "tp"), P("tp", ("ctx", "dp")), P(),
    )
    return jax.shard_map(
        on_device, mesh=mesh, in_specs=placed, out_specs=(P("dp", "ctx", "tp"), P()), check_vma=False
    )
```

time: 128 us -> 110 us (0.86)
  Pallas kernels: 123 us -> 107 us
  local copies, waits for them, and re-layouts: 2.26 us -> 0.97 us
    pallas_call x1, Pallas kernels: 123 us -> 107 us  [on_device(): pl.pallas_call(layer_kernel, out_shape=(pltpu.VMEM((512, 1024), bf16), ja...]
    unnamed x1, local copies, waits for them, and re-layouts: 2.26 us -> 0.97 us
where the time goes in v3:
time: 110 us
  Pallas kernels  107 us (97%)
  between operations  2.33 us (2%)
    pallas_call x1, Pallas kernels, on_device(): pl.pallas_call(layer_kernel, out_shape=(pltpu.VMEM((512, 1024), bf16), ja...  107 us

profile of v3, /device:TPU:1, one launch (start us, length us, event | category | flops | bytes accessed | tf_op | source)
XLA Modules:
  0.0 109.9 jit_solution(8147094558358774406)
XLA Ops:
  0.6 106.6 %layer.1 = (bf16[512,1024]{1,0:T(8,128)(2,1)S(1)}, f32[1,1]{1,0:T(1,128)}) custom-call(bf16[1,512,1024]{2,1,0:T(8,128)(2,1)} %hid.1, bf16[1,512,1024]{2,1,0:T(8,128)(2,1)} %tgt.1, bf16[128,512]{1,0:T(8,128)(2,1)} %wq.1, bf16[128,128]{1,0:T(8,128)(2,1)} %wk.1, bf16[128,128]{1,0:T(8,128)(2,1)} %wv.1, bf16[512,128]{1,0:T(8,128)(2,1)} %wo.1, f32[1,4096]{1,0:T(1,128)} %bitcast.4, ...), custom_call_target="tpu_custom_call" | custom-call | tf_op jit(solution)/shard_map/layer/pallas_call | solution.py:600
  107.3 1.0 copy.16

commit v4 on v3

--- a/solution.py
+++ b/solution.py
@@ -95,7 +95,7 @@
 def layer_kernel(
     hid, tgt, wq, wk, wv, wo, gain, order, turn_cos, turn_sin, block_cos, block_sin,
     out, loss_out,
-    H, N, RH, W, acc, Q, KV, WO, AT, RA, num, peak, T, total, LB, row_cos, row_sin, ssem, rsem, lsem, osend, orecv,
+    H, N, RH, W, acc, Q, KV, WO, AT, RA, num, peak, T, total, LB, row_cos, row_sin, ssem, rsem, lsem, osend, orecv, zsend, zrecv,
 ):
     m = places()
     net = Net(ssem, rsem)
@@ -219,7 +219,7 @@
 
     def along(k, ref, s):
         return pltpu.make_async_remote_copy(
-            src_ref=ref, dst_ref=ref, send_sem=osend.at[k], recv_sem=orecv.at[k],
+            src_ref=ref, dst_ref=ref, send_sem=zsend.at[k], recv_sem=zrecv.at[k],
             device_id=m.Z[s], device_id_type=MESH,
         )
 
@@ -238,8 +238,10 @@
                     device_id=(c, m.z, d), device_id_type=MESH,
                 ).wait_recv()
 
-        along(0, mine, 1).start()
-        along(1, mine, -1).start()
+        along(0, low, 1).start()
+        along(1, high, -1).start()
+        along(4, high, 1).start()
+        along(5, low, -1).start()
 
     def strip(xl, y, s=None):
         return WO.at[xl * 4 + y] if s is None else WO.at[xl * 4 + y, pl.ds(0 if s == 1 else 1024, 1024)]
@@ -324,6 +326,16 @@
             lax.fori_loop(0, 256 // step, rope, 0)
 
     rotate((4,))
+    @pl.when(turn == 1)
+    def _():
+        along(0, low, 1).wait_recv()
+        along(2, low, 1).start()
+
+    @pl.when(turn == 3)
+    def _():
+        along(1, high, -1).wait_recv()
+        along(3, high, -1).start()
+
     kv0 = net.send(KV.at[c], m.P)
     kv1 = {s: net.send(KV.at[c], m.Z[s]) for s in SIDES}
 
@@ -336,15 +348,15 @@
 
     acc[:, pl.ds(0, 256)] = columns((m.z, m.zo[1], m.zo[-1], m.z2), 0)
 
+    acc[:, pl.ds(256, 256)] = columns((m.z, m.zo[1], m.zo[-1], m.z2), 256)
+
     @pl.when(turn == 1)
     def _():
-        along(0, mine, 1).wait_recv()
-        along(2, low, 1).start()
+        along(4, high, 1).wait_recv()
 
     @pl.when(turn == 3)
     def _():
-        along(1, mine, -1).wait_recv()
-        along(3, high, -1).start()
+        along(5, low, -1).wait_recv()
 
     @pl.when(turn % 2 == 1)
     def _():
@@ -353,7 +365,6 @@
         for s in SIDES:
             net.start(wo0[s])
 
-    acc[:, pl.ds(256, 256)] = columns((m.z, m.zo[1], m.zo[-1], m.z2), 256)
     rotate((0, 1, 2, 3))
 
     def bias(s, ctx, half):
@@ -411,30 +422,33 @@
                 out.append((at, tile(h, s, at, size, ctxs, first, lift)))
         return out
 
-    def attend(ctxs, first=False):
+    def attend(ctxs, first=False, between=None):
         lift = lifts(ctxs, first)
         for h in range(4):
+            if between is not None and h == 2:
+                between()
             for at, (new, part) in tiles(h, ctxs, first, lift):
                 peak[h, at, :], num[h, at, :] = new, part
 
     kv2, kv3, kv4, kv5, wo2, wo3, wo4 = {}, {}, {}, {}, {}, {}, {}
     part_of = {1: 0, -1: 1}
     both, early, late = pl.ds(0, 2), pl.ds(0, 320), pl.ds(320, 192)
-    attend((c,), True)
-
-    @pl.when(turn == 2)
-    def _():
-        along(2, low, 1).wait_recv()
-        along(3, high, -1).wait_recv()
-        for s in SIDES:
-            net.start(wo1[s])
-        for s in SIDES:
-            net.start(wo0[s])
-
-
-    net.recv(kv0, KV.at[m.c1])
-    for s in SIDES:
-        kv2[s] = net.send(KV.at[m.c1, both, early], m.Z[s])
+    def to_z():
+        net.recv(kv0, KV.at[m.c1])
+        for s in SIDES:
+            kv2[s] = net.send(KV.at[m.c1, both, early], m.Z[s])
+
+        @pl.when(turn == 2)
+        def _():
+            along(2, low, 1).wait_recv()
+            along(3, high, -1).wait_recv()
+            for s in SIDES:
+                net.start(wo1[s])
+            for s in SIDES:
+                net.start(wo0[s])
+
+    attend((c,), True, to_z)
+
     for s in SIDES:
         there = 2 * m.zo[s] + m.xl
         net.recv(kv1[s], KV.at[there])
@@ -449,8 +463,11 @@
             net.recv(wo1[s], strip(m.xl, m.yo[s]))
             net.start(wo3[s])
 
+    @pl.when(turn == 0)
+    def _():
+        pass_on()
+
     attend((m.c1,))
-    pass_on()
     for s in SIDES:
         there = 2 * m.zo[s] + m.xo
         net.recv(kv2[s], KV.at[there, both, early])
@@ -458,7 +475,6 @@
     for s in SIDES:
         net.recv(kv3[s], KV.at[2 * m.z2 + m.xl, part_of[s]])
     kv6 = net.send(KV.at[2 * m.z2 + m.xl, both, late], m.P)
-    attend((2 * m.z2 + m.xl,))
     for r in SIDES:
         for s in SIDES:
             wo2[r, s] = net.plan(strip(m.xo, d, r), m.Y[s])
@@ -469,10 +485,25 @@
             for s in SIDES:
                 net.start(wo2[r, s])
 
-    cross()
+    @pl.when(turn % 2 == 1)
+    def _():
+        pass_on()
+
+    attend((2 * m.z2 + m.xl,))
+
+    @pl.when(turn != 2)
+    def _():
+        cross()
+
     for s in SIDES:
         net.recv(kv5[s], KV.at[2 * m.zo[s] + m.xo, both, late])
     attend([2 * m.zo[s] + m.xo for s in SIDES])
+
+    @pl.when(turn == 2)
+    def _():
+        pass_on()
+        cross()
+
 
     for s in SIDES:
         net.recv(kv4[s], KV.at[2 * m.z2 + m.xo, part_of[s], early])
@@ -488,16 +519,26 @@
         ks = [net.send(AT.at[t, h, pl.ds(s * 256, 256)], (m.P, m.Q)[s], RA.at[s, h]) for s in range(2)]
         ks.append(net.send(AT.at[t, h], m.C))
         kA.append(ks)
+    for s in SIDES:
+        wo4[s] = net.plan(strip(m.xo, m.yo[s], s), m.Y[s])
+
+    def hop(now):
+        @pl.when(now)
+        def _():
+            for s in SIDES:
+                net.recv(wo2[s, s], strip(m.xo, m.yo[s], s))
+                net.start(wo4[s])
+
+    hop(turn == 0)
     kR = []
     for h in range(4):
         net.recv(kA[h][0], RA.at[0, h])
         a = net.send(RA.at[0, h], m.Q, AT.at[t, h, top])
         net.recv(kA[h][1], RA.at[1, h])
         kR.append((a, net.send(RA.at[1, h], m.P, AT.at[m.t2, h, bottom])))
-        if h == 3:
-            for s in SIDES:
-                net.recv(wo2[s, s], strip(m.xo, m.yo[s], s))
-                wo4[s] = net.send(strip(m.xo, m.yo[s], s), m.Y[s])
+        if h == 1:
+            hop(turn % 2 == 1)
+    hop(turn == 2)
     kD = []
     for h in range(4):
         net.recv(kR[h][0], AT.at[m.t2, h, top])
@@ -579,7 +620,7 @@
     def _():
         meet(t).wait_send()
 
-    for k, ref, s, when in ((0, mine, 1, 0), (1, mine, -1, 0), (2, low, 1, 1), (3, high, -1, 3)):
+    for k, ref, s, when in ((0, low, 1, 0), (1, high, -1, 0), (4, high, 1, 0), (5, low, -1, 0), (2, low, 1, 1), (3, high, -1, 3)):
         @pl.when(turn == when)
         def _(k=k, ref=ref, s=s):
             along(k, ref, s).wait_send()
@@ -625,6 +666,8 @@
             pltpu.SemaphoreType.DMA((8,)),
             pltpu.SemaphoreType.DMA((8,)),
             pltpu.SemaphoreType.DMA((10,)),
+            pltpu.SemaphoreType.DMA((6,)),
+            pltpu.SemaphoreType.DMA((6,)),
         ],
         compiler_params=pltpu.CompilerParams(
             collective_id=0, has_side_effects=True, vmem_limit_bytes=60 * MIB

time: 110 us -> 109 us (level)
  no operation moved by 1% of the time
where the time goes in v4:
time: 109 us
  Pallas kernels  106 us (97%)
  between operations  2.33 us (2%)
    pallas_call x1, Pallas kernels, on_device(): pl.pallas_call(layer_kernel, out_shape=(pltpu.VMEM((512, 1024), bf16), ja...  106 us

profile of v4, /device:TPU:1, one launch (start us, length us, event | category | flops | bytes accessed | tf_op | source)
XLA Modules:
  0.0 109.0 jit_solution(5319070870002870077)
XLA Ops:
  0.6 105.7 %layer.1 = (bf16[512,1024]{1,0:T(8,128)(2,1)S(1)}, f32[1,1]{1,0:T(1,128)}) custom-call(bf16[1,512,1024]{2,1,0:T(8,128)(2,1)} %hid.1, bf16[1,512,1024]{2,1,0:T(8,128)(2,1)} %tgt.1, bf16[128,512]{1,0:T(8,128)(2,1)} %wq.1, bf16[128,128]{1,0:T(8,128)(2,1)} %wk.1, bf16[128,128]{1,0:T(8,128)(2,1)} %wv.1, bf16[512,128]{1,0:T(8,128)(2,1)} %wo.1, f32[1,4096]{1,0:T(1,128)} %bitcast.4, ...), custom_call_target="tpu_custom_call" | custom-call | tf_op jit(solution)/shard_map/layer/pallas_call | solution.py:641
  106.4 1.0 copy.16

commit v5 on v4

--- a/solution.py
+++ b/solution.py
@@ -14,8 +14,8 @@
 NEG = -1e30
 SCALE = float(np.log2(np.e) / np.sqrt(HEAD_SIZE))
 MIB = 1024 * 1024
-POOL = 40
-COPIES = 120
+POOL = 64
+COPIES = 112
 
 MESH = pl.DeviceIdType.MESH
 SIDES = (1, -1)
@@ -430,13 +430,12 @@
             for at, (new, part) in tiles(h, ctxs, first, lift):
                 peak[h, at, :], num[h, at, :] = new, part
 
-    kv2, kv3, kv4, kv5, wo2, wo3, wo4 = {}, {}, {}, {}, {}, {}, {}
+    kv2, kv3, kv4, wo2, wo3, wo4 = {}, {}, {}, {}, {}, {}
     part_of = {1: 0, -1: 1}
-    both, early, late = pl.ds(0, 2), pl.ds(0, 320), pl.ds(320, 192)
     def to_z():
         net.recv(kv0, KV.at[m.c1])
         for s in SIDES:
-            kv2[s] = net.send(KV.at[m.c1, both, early], m.Z[s])
+            kv2[s] = net.send(KV.at[m.c1], m.Z[s])
 
         @pl.when(turn == 2)
         def _():
@@ -453,7 +452,6 @@
         there = 2 * m.zo[s] + m.xl
         net.recv(kv1[s], KV.at[there])
         kv3[s] = net.send(KV.at[there, part_of[s]], m.Z[s])
-        kv5[s] = net.send(KV.at[there, both, late], m.P)
     attend([2 * m.zo[s] + m.xl for s in SIDES])
     for s in SIDES:
         wo3[s] = net.plan(strip(m.xl, m.yo[s], s), m.Y[s])
@@ -470,11 +468,10 @@
     attend((m.c1,))
     for s in SIDES:
         there = 2 * m.zo[s] + m.xo
-        net.recv(kv2[s], KV.at[there, both, early])
-        kv4[s] = net.send(KV.at[there, part_of[s], early], m.Z[s])
+        net.recv(kv2[s], KV.at[there])
+        kv4[s] = net.send(KV.at[there, part_of[s]], m.Z[s])
     for s in SIDES:
         net.recv(kv3[s], KV.at[2 * m.z2 + m.xl, part_of[s]])
-    kv6 = net.send(KV.at[2 * m.z2 + m.xl, both, late], m.P)
     for r in SIDES:
         for s in SIDES:
             wo2[r, s] = net.plan(strip(m.xo, d, r), m.Y[s])
@@ -495,8 +492,6 @@
     def _():
         cross()
 
-    for s in SIDES:
-        net.recv(kv5[s], KV.at[2 * m.zo[s] + m.xo, both, late])
     attend([2 * m.zo[s] + m.xo for s in SIDES])
 
     @pl.when(turn == 2)
@@ -506,8 +501,7 @@
 
 
     for s in SIDES:
-        net.recv(kv4[s], KV.at[2 * m.z2 + m.xo, part_of[s], early])
-    net.recv(kv6, KV.at[2 * m.z2 + m.xo, both, late])
+        net.recv(kv4[s], KV.at[2 * m.z2 + m.xo, part_of[s]])
 
     last = (2 * m.z2 + m.xo,)
     lift = lifts(last)
@@ -538,13 +532,6 @@
         kR.append((a, net.send(RA.at[1, h], m.P, AT.at[m.t2, h, bottom])))
         if h == 1:
             hop(turn % 2 == 1)
-    hop(turn == 2)
-    kD = []
-    for h in range(4):
-        net.recv(kR[h][0], AT.at[m.t2, h, top])
-        net.recv(kR[h][1], AT.at[m.t2, h, bottom])
-        kD.append(net.send(AT.at[m.t2, h], m.C))
-
     soon = [[(m.xl, d), (m.xl, m.yo[1])], [(m.xl, m.yo[-1]), (m.xl, m.y2)], [(m.xo, d), (m.xo, m.yo[1])]]
     last_two = [(m.xo, m.yo[-1]), (m.xo, m.y2)]
 
@@ -555,8 +542,8 @@
         )
         return jnp.dot(left, right, preferred_element_type=jnp.float32)
 
-    def project(bs, first=False):
-        for two in soon:
+    def project(bs, twos, first=False):
+        for two in twos:
             part = product(bs, two)
             for i, (xl, y) in enumerate(two):
                 cols = pl.ds(pl.multiple_of((xl * 4 + y) * 128, 128), 128)
@@ -566,36 +553,51 @@
                 else:
                     total[:, cols] += piece
 
+    for h in range(4):
+        net.recv(kA[h][2], AT.at[m.t1, h])
+    project((t, m.t1), soon[:1], True)
+    kD = []
+    for h in range(4):
+        net.recv(kR[h][0], AT.at[m.t2, h, top])
+        net.recv(kR[h][1], AT.at[m.t2, h, bottom])
+        kD.append(net.send(AT.at[m.t2, h], m.C))
+    hop(turn == 2)
+
     for s in SIDES:
         net.recv(wo3[s], strip(m.xl, m.y2, s))
     net.recv(wo2[-1, 1], strip(m.xo, m.yo[1], -1))
     net.recv(wo2[1, -1], strip(m.xo, m.yo[-1], 1))
-    for h in range(4):
-        net.recv(kA[h][2], AT.at[m.t1, h])
-    project((t, m.t1), True)
-    project((m.t2,))
+    project((t, m.t1), soon[1:], True)
+    project((m.t2,), soon)
     for h in range(4):
         net.recv(kD[h], AT.at[m.t3, h])
-    project((m.t3,))
+    project((m.t3,), soon)
+    later.wait()
+
+    def close(two, part):
+        for xl, y in two:
+            cols = pl.ds(pl.multiple_of((xl * 4 + y) * 128, 128), 128)
+            for i in range(4):
+                at = pl.ds(i * 128, 128)
+                branch = total[at, cols].astype(jnp.bfloat16)
+                out[at, cols] = branch
+                gap = H[t, at, cols].astype(jnp.float32) + branch.astype(jnp.float32) - T[at, cols].astype(jnp.float32)
+                sq = gap * gap
+                fold = [sq[r * 8 : (r + 1) * 8] for r in range(16)]
+                while len(fold) > 1:
+                    fold = [a + b for a, b in zip(fold[::2], fold[1::2])]
+                part = part + fold[0]
+        return part
+
+    part = jnp.zeros((8, 128), jnp.float32)
+    for two in soon:
+        part = close(two, part)
     for s in SIDES:
         net.recv(wo4[s], strip(m.xo, m.y2, s))
-    part = product((t, m.t1, m.t2, m.t3), last_two)
+    rest = product((t, m.t1, m.t2, m.t3), last_two)
     for i, (xl, y) in enumerate(last_two):
-        total[:, pl.ds(pl.multiple_of((xl * 4 + y) * 128, 128), 128)] = part[:, i * 128 : (i + 1) * 128]
-    later.wait()
-
-    def close(i, carry):
-        at = pl.ds(pl.multiple_of(i * 32, 32), 32)
-        branch = total[at, :].astype(jnp.bfloat16)
-        out[at, :] = branch
-        gap = H[t, at, :].astype(jnp.float32) + branch.astype(jnp.float32) - T[at, :].astype(jnp.float32)
-        sq = gap * gap
-        for r in range(4):
-            for b in range(8):
-                carry = carry + sq[r * 8 : (r + 1) * 8, b * 128 : (b + 1) * 128]
-        return carry
-
-    part = lax.fori_loop(0, 16, close, jnp.zeros((8, 128), jnp.float32))
+        total[:, pl.ds(pl.multiple_of((xl * 4 + y) * 128, 128), 128)] = rest[:, i * 128 : (i + 1) * 128]
+    part = close(last_two, part)
     rings = (
         (8, m.xl * 4 + t, lambda i: (2 * m.z + i // 4, i % 4, d)),
         (16, m.z * 4 + d, lambda i: (2 * (i // 4) + m.xl, t, i % 4)),

time: 109 us -> 109 us (level)
  no operation moved by 1% of the time
where the time goes in v5:
time: 109 us; the launch traced here: 108 us
  Pallas kernels  105 us (96%)
  between operations  2.33 us (2%)
    pallas_call x1, Pallas kernels, on_device(): pl.pallas_call(layer_kernel, out_shape=(pltpu.VMEM((512, 1024), bf16), ja...  105 us

profile of v5, /device:TPU:1, one launch (start us, length us, event | category | flops | bytes accessed | tf_op | source)
XLA Modules:
  0.0 108.5 jit_solution(10016761373667571179)
XLA Ops:
  0.6 105.2 %layer.1 = (bf16[512,1024]{1,0:T(8,128)(2,1)S(1)}, f32[1,1]{1,0:T(1,128)}) custom-call(bf16[1,512,1024]{2,1,0:T(8,128)(2,1)} %hid.1, bf16[1,512,1024]{2,1,0:T(8,128)(2,1)} %tgt.1, bf16[128,512]{1,0:T(8,128)(2,1)} %wq.1, bf16[128,128]{1,0:T(8,128)(2,1)} %wk.1, bf16[128,128]{1,0:T(8,128)(2,1)} %wv.1, bf16[512,128]{1,0:T(8,128)(2,1)} %wo.1, f32[1,4096]{1,0:T(1,128)} %bitcast.4, ...), custom_call_target="tpu_custom_call" | custom-call | tf_op jit(solution)/shard_map/layer/pallas_call | solution.py:643
  105.8 1.0 copy.16

commit v6 on v5

--- a/solution.py
+++ b/solution.py
@@ -530,8 +530,6 @@
         a = net.send(RA.at[0, h], m.Q, AT.at[t, h, top])
         net.recv(kA[h][1], RA.at[1, h])
         kR.append((a, net.send(RA.at[1, h], m.P, AT.at[m.t2, h, bottom])))
-        if h == 1:
-            hop(turn % 2 == 1)
     soon = [[(m.xl, d), (m.xl, m.yo[1])], [(m.xl, m.yo[-1]), (m.xl, m.y2)], [(m.xo, d), (m.xo, m.yo[1])]]
     last_two = [(m.xo, m.yo[-1]), (m.xo, m.y2)]
 
@@ -561,6 +559,8 @@
         net.recv(kR[h][0], AT.at[m.t2, h, top])
         net.recv(kR[h][1], AT.at[m.t2, h, bottom])
         kD.append(net.send(AT.at[m.t2, h], m.C))
+        if h == 1:
+            hop(turn % 2 == 1)
     hop(turn == 2)
 
     for s in SIDES:

time: 109 us -> 109 us (level)
  no operation moved by 1% of the time
where the time goes in v6:
time: 109 us; the launch traced here: 108 us
  Pallas kernels  105 us (96%)
  between operations  2.33 us (2%)
    pallas_call x1, Pallas kernels, on_device(): pl.pallas_call(layer_kernel, out_shape=(pltpu.VMEM((512, 1024), bf16), ja...  105 us

profile of v6, /device:TPU:1, one launch (start us, length us, event | category | flops | bytes accessed | tf_op | source)
XLA Modules:
  0.0 108.4 jit_solution(2255193995357231654)
XLA Ops:
  0.6 105.1 %layer.1 = (bf16[512,1024]{1,0:T(8,128)(2,1)S(1)}, f32[1,1]{1,0:T(1,128)}) custom-call(bf16[1,512,1024]{2,1,0:T(8,128)(2,1)} %hid.1, bf16[1,512,1024]{2,1,0:T(8,128)(2,1)} %tgt.1, bf16[128,512]{1,0:T(8,128)(2,1)} %wq.1, bf16[128,128]{1,0:T(8,128)(2,1)} %wk.1, bf16[128,128]{1,0:T(8,128)(2,1)} %wv.1, bf16[512,128]{1,0:T(8,128)(2,1)} %wo.1, f32[1,4096]{1,0:T(1,128)} %bitcast.4, ...), custom_call_target="tpu_custom_call" | custom-call | tf_op jit(solution)/shard_map/layer/pallas_call | solution.py:643
  105.7 1.0 copy.16

commit v7 on v6

--- a/solution.py
+++ b/solution.py
@@ -15,7 +15,7 @@
 SCALE = float(np.log2(np.e) / np.sqrt(HEAD_SIZE))
 MIB = 1024 * 1024
 POOL = 64
-COPIES = 112
+COPIES = 118
 
 MESH = pl.DeviceIdType.MESH
 SIDES = (1, -1)
@@ -130,7 +130,7 @@
     parts = 4
     rows = 256 // parts
 
-    kX = net.send(W.at[c, d], m.P)
+    kX = [net.send(W.at[c, d, at], m.P) for at in (ha, hb)]
     kY1 = {s: net.send(W.at[c, d], m.Y[s]) for s in SIDES}
     kZ1 = {s: net.send(W.at[c, d], m.Z[s]) for s in SIDES}
     kH0 = [net.send(H.at[t, pl.ds(i * rows, rows)], m.P, RH.at[0, pl.ds(i * rows, rows)]) for i in range(parts)]
@@ -154,9 +154,12 @@
     def _():
         meet(t).start()
 
-    net.recv(kX, W.at[m.c1, d])
-    kY2 = {s: net.send(W.at[m.c1, d], m.Y[s]) for s in SIDES}
-    kZ2 = {s: net.send(W.at[m.c1, d], m.Z[s]) for s in SIDES}
+    kY2, kZ2 = {}, {}
+    for i, at in enumerate((ha, hb)):
+        net.recv(kX[i], W.at[m.c1, d, at])
+        for s in SIDES:
+            kY2[s, i] = net.send(W.at[m.c1, d, at], m.Y[s])
+            kZ2[s, i] = net.send(W.at[m.c1, d, at], m.Z[s])
 
     def relay(i):
         net.recv(kH0[i], RH.at[0, pl.ds(i * rows, rows)])
@@ -179,9 +182,11 @@
         net.recv(kZ1[s], W.at[2 * m.zo[s] + m.xl, d])
     kF.append(relay(0))
     for s in SIDES:
-        net.recv(kY2[s], W.at[m.c1, m.yo[s]])
+        for i, at in enumerate((ha, hb)):
+            net.recv(kY2[s, i], W.at[m.c1, m.yo[s], at])
         kY3[s] = net.send(W.at[pair(m.z), m.yo[s], qa[s]], m.Y[s])
-        net.recv(kZ2[s], W.at[2 * m.zo[s] + m.xo, d])
+        for i, at in enumerate((ha, hb)):
+            net.recv(kZ2[s, i], W.at[2 * m.zo[s] + m.xo, d, at])
         kZ3[s] = net.send(W.at[pair(m.zo[s]), d, qb[s]], m.Z[s])
     for s in SIDES:
         for r in SIDES:

time: 109 us -> 107 us (0.982)
  no operation moved by 1% of the time
where the time goes in v7:
time: 107 us
  Pallas kernels  104 us (97%)
  between operations  2.33 us (2%)
    pallas_call x1, Pallas kernels, on_device(): pl.pallas_call(layer_kernel, out_shape=(pltpu.VMEM((512, 1024), bf16), ja...  104 us

profile of v7, /device:TPU:1, one launch (start us, length us, event | category | flops | bytes accessed | tf_op | source)
XLA Modules:
  0.0 107.3 jit_solution(3618336182659126063)
XLA Ops:
  0.6 104.0 %layer.1 = (bf16[512,1024]{1,0:T(8,128)(2,1)S(1)}, f32[1,1]{1,0:T(1,128)}) custom-call(bf16[1,512,1024]{2,1,0:T(8,128)(2,1)} %hid.1, bf16[1,512,1024]{2,1,0:T(8,128)(2,1)} %tgt.1, bf16[128,512]{1,0:T(8,128)(2,1)} %wq.1, bf16[128,128]{1,0:T(8,128)(2,1)} %wk.1, bf16[128,128]{1,0:T(8,128)(2,1)} %wv.1, bf16[512,128]{1,0:T(8,128)(2,1)} %wo.1, f32[1,4096]{1,0:T(1,128)} %bitcast.4, ...), custom_call_target="tpu_custom_call" | custom-call | tf_op jit(solution)/shard_map/layer/pallas_call | solution.py:648
  104.7 1.0 copy.16
